TPU v7x, 8 devices: a whole 2x2x1 slice. The times are simulated.
8 devices in a mesh: cp: 8 (over z, y, x, core).
Axes of the slice: x: 2, y: 2, z: 1, core: 2. Of those that a mesh axis runs over, the one named last changes fastest.
Arguments:
- x_in: bfloat16 [8192, 640], P('cp')
- norm_gains: float32 [2, 4, 640], replicated
- qk_gains: float32 [2, 2, 256], replicated
- w_q: bfloat16 [2, 640, 4, 256], replicated
- w_k: bfloat16 [2, 640, 1, 256], replicated
- w_v: bfloat16 [2, 640, 1, 256], replicated
- w_o: bfloat16 [2, 4, 256, 640], replicated
- w_gate: bfloat16 [2, 640, 2048], replicated
- w_up: bfloat16 [2, 640, 2048], replicated
- w_down: bfloat16 [2, 2048, 640], replicated
Outputs:
- output 1: bfloat16 [8192, 640], P('cp')
- output 2: bfloat16 [8192, 1, 256], P('cp')
- output 3: bfloat16 [8192, 1, 256], P('cp')
- output 4: bfloat16 [1024, 1, 256], replicated
- output 5: bfloat16 [1024, 1, 256], replicated
All inputs are finite; a program needn't handle non-finite values.
Results may differ from a plain program's by a relative error of at most 0.016197.
Values are sent between devices in bfloat16 or wider.
A program may use at most 1 GiB of HBM per device.

v0:
```python
import jax
import jax.numpy as jnp
from jax import lax
from jax.sharding import PartitionSpec as P

WINDOW = 1024
EPS = 1e-6
LOCAL_BASE = 10000.0
GLOBAL_BASE = 1000000.0
GLOBAL_SCALE = 8.0


def gain_norm(x_val, gain_vec):
    x_f32 = x_val.astype(jnp.float32)
    mean_sq = jnp.mean(x_f32 * x_f32, axis=-1, keepdims=True)
    return x_f32 * lax.rsqrt(mean_sq + EPS) * (1.0 + gain_vec)


def rope_tables(positions, head_dim, rope_base, pos_scale):
    inv_freq = rope_base ** (-jnp.arange(head_dim // 2, dtype=jnp.float32) * 2.0 / head_dim)
    angles = (positions.astype(jnp.float32) / pos_scale)[:, None] * inv_freq[None, :]
    return jnp.cos(angles), jnp.sin(angles)


def rotate(x_val, cos_tab, sin_tab):
    half_dim = x_val.shape[-1] // 2
    lower_half = x_val[..., :half_dim]
    upper_half = x_val[..., half_dim:]
    return jnp.concatenate([lower_half * cos_tab - upper_half * sin_tab, upper_half * cos_tab + lower_half * sin_tab], axis=-1)


def project(x_blk, layer_gains, qk_gain, w_q, w_k, w_v, positions, rope_base, pos_scale):
    d_model, n_heads, head_dim = w_q.shape
    kv_heads = w_k.shape[1]
    normed = gain_norm(x_blk, layer_gains[0]).astype(jnp.bfloat16)
    w_q_split = w_q.reshape(d_model, kv_heads, n_heads // kv_heads, head_dim)
    q_proj = jnp.einsum('tm,mkge->kgte', normed, w_q_split, preferred_element_type=jnp.float32).astype(jnp.bfloat16)
    k_proj = jnp.einsum('tm,mke->tke', normed, w_k, preferred_element_type=jnp.float32).astype(jnp.bfloat16)
    v_proj = jnp.einsum('tm,mke->tke', normed, w_v, preferred_element_type=jnp.float32).astype(jnp.bfloat16)
    cos_tab, sin_tab = rope_tables(positions, head_dim, rope_base, pos_scale)
    q_rot = rotate(gain_norm(q_proj, qk_gain[0]), cos_tab, sin_tab).astype(jnp.bfloat16)
    k_rot = rotate(gain_norm(k_proj, qk_gain[1]), cos_tab[:, None, :], sin_tab[:, None, :]).astype(jnp.bfloat16)
    return q_rot, k_rot, v_proj


def finish(x_blk, attn_out, layer_gains, w_o, w_gate, w_up, w_down):
    kv_heads, n_group = attn_out.shape[0], attn_out.shape[1]
    head_dim, d_model = w_o.shape[1], w_o.shape[2]
    w_o_split = w_o.reshape(kv_heads, n_group, head_dim, d_model)
    o_proj = jnp.einsum('kgtd,kgdm->tm', attn_out, w_o_split, preferred_element_type=jnp.float32).astype(jnp.bfloat16)
    resid_mid = (x_blk.astype(jnp.float32) + gain_norm(o_proj, layer_gains[1])).astype(jnp.bfloat16)
    ff_in = gain_norm(resid_mid, layer_gains[2]).astype(jnp.bfloat16)
    gate_act = jnp.dot(ff_in, w_gate, preferred_element_type=jnp.float32)
    up_proj = jnp.dot(ff_in, w_up, preferred_element_type=jnp.float32)
    hidden = (jax.nn.gelu(gate_act, approximate=True) * up_proj).astype(jnp.bfloat16)
    mlp_out = jnp.dot(hidden, w_down, preferred_element_type=jnp.float32).astype(jnp.bfloat16)
    return (resid_mid.astype(jnp.float32) + gain_norm(mlp_out, layer_gains[3])).astype(jnp.bfloat16)


def local_attend(q_rot, k_win, v_win, q_pos, k_pos):
    scores = jnp.einsum('kgte,ske->kgts', q_rot, k_win, preferred_element_type=jnp.float32) * q_rot.shape[-1] ** -0.5
    offsets = q_pos[:, None] - k_pos[None, :]
    visible = (offsets >= 0) & (offsets < WINDOW) & (k_pos >= 0)[None, :]
    scores = jnp.where(visible, scores, -jnp.inf)
    exp_scores = jnp.exp(scores - scores.max(axis=-1, keepdims=True))
    prob_sum = exp_scores.sum(axis=-1, keepdims=True)
    weighted = jnp.einsum('kgts,ske->kgte', exp_scores.astype(jnp.bfloat16), v_win, preferred_element_type=jnp.float32)
    return (weighted / prob_sum).astype(jnp.bfloat16)


def merge_block(soft_state, q_rot, k_blk, v_blk, q_pos, k_pos):
    run_max, run_sum, run_acc = soft_state
    scores = jnp.einsum('kgte,ske->kgts', q_rot, k_blk, preferred_element_type=jnp.float32) * q_rot.shape[-1] ** -0.5
    scores = jnp.where(q_pos[:, None] >= k_pos[None, :], scores, -jnp.inf)
    new_max = jnp.maximum(run_max, scores.max(axis=-1))
    exp_scores = jnp.exp(scores - new_max[..., None])
    decay_fac = jnp.exp(run_max - new_max)
    new_sum = decay_fac * run_sum + exp_scores.sum(axis=-1)
    new_acc = decay_fac[..., None] * run_acc + jnp.einsum('kgts,ske->kgte', exp_scores.astype(jnp.bfloat16), v_blk, preferred_element_type=jnp.float32)
    return new_max, new_sum, new_acc


def solution(mesh):
    n_dev = mesh.shape['cp']
    shift_perm = [(sender, (sender + 1) % n_dev) for sender in range(n_dev)]

    def shard_body(x_blk, norm_gains, qk_gains, w_q, w_k, w_v, w_o, w_gate, w_up, w_down):
        tokens = x_blk.shape[0]
        seq_len = tokens * n_dev
        my_index = lax.axis_index('cp')
        positions = my_index * tokens + jnp.arange(tokens)
        q_loc, k_loc, v_loc = project(x_blk, norm_gains[0], qk_gains[0], w_q[0], w_k[0], w_v[0], positions, LOCAL_BASE, 1.0)
        own_kv = jnp.stack([k_loc, v_loc])
        tail_len = min(WINDOW, tokens)
        tail_rows = own_kv[:, tokens - tail_len:]
        pieces = [own_kv]
        for hop_dist in range(1, WINDOW // tail_len + 1):
            if hop_dist < n_dev:
                received = lax.ppermute(tail_rows, 'cp', perm=[(sender, sender + hop_dist) for sender in range(n_dev - hop_dist)])
            else:
                received = jnp.zeros_like(tail_rows)
            pieces = [received] + pieces
        window_kv = jnp.concatenate(pieces, axis=1)
        key_pos = positions[0] - WINDOW + jnp.arange(WINDOW + tokens)
        attn_loc = local_attend(q_loc, window_kv[0], window_kv[1], positions, key_pos)
        mid_out = finish(x_blk, attn_loc, norm_gains[0], w_o[0], w_gate[0], w_up[0], w_down[0])
        zero_rows = jnp.zeros((2, WINDOW) + own_kv.shape[2:], own_kv.dtype)
        extended = jnp.concatenate([zero_rows, own_kv, zero_rows], axis=1)
        rel_start = my_index * tokens - (seq_len - WINDOW)
        placed = lax.dynamic_slice_in_dim(extended, WINDOW - rel_start, WINDOW, axis=1)
        local_kv = lax.psum(placed, 'cp')
        q_glob, k_glob, v_glob = project(mid_out, norm_gains[1], qk_gains[1], w_q[1], w_k[1], w_v[1], positions, GLOBAL_BASE, GLOBAL_SCALE)
        kv_heads, n_group, head_dim = q_glob.shape[0], q_glob.shape[1], q_glob.shape[3]
        init_state = (jnp.full((kv_heads, n_group, tokens), -jnp.inf, jnp.float32), jnp.zeros((kv_heads, n_group, tokens), jnp.float32), jnp.zeros((kv_heads, n_group, tokens, head_dim), jnp.float32))
        soft_state = merge_block(init_state, q_glob, k_glob, v_glob, positions, positions)

        def step_fn(step_num, loop_carry):
            held_kv, run_state = loop_carry
            held_kv = lax.ppermute(held_kv, 'cp', perm=shift_perm)
            blk_pos = (my_index - step_num) * tokens + jnp.arange(tokens)
            run_state = lax.cond(step_num <= my_index, lambda prior: merge_block(prior, q_glob, held_kv[0], held_kv[1], positions, blk_pos), lambda prior: prior, run_state)
            return held_kv, run_state

        last_held, soft_state = lax.fori_loop(1, n_dev, step_fn, (jnp.stack([k_glob, v_glob]), soft_state))
        attn_glob = (soft_state[2] / soft_state[1][..., None]).astype(jnp.bfloat16)
        x_out = finish(mid_out, attn_glob, norm_gains[1], w_o[1], w_gate[1], w_up[1], w_down[1])
        return x_out, k_glob, v_glob, local_kv[0], local_kv[1]

    return jax.shard_map(shard_body, mesh=mesh, in_specs=(P('cp'), P(), P(), P(), P(), P(), P(), P(), P(), P()), out_specs=(P('cp'), P('cp'), P('cp'), P(), P()), check_vma=False)
```

profile of v0, /device:TPU:7, one launch (start us, length us, event | category | flops | bytes accessed | tf_op | source)
XLA Modules:
  0.0 420.5 jit_solution(2442085099498469903)
XLA Ops:
  46.0 22.8 %all-reduce.2.cloned.1.call-done = bf16[2,1024,1,256]{1,3,2,0:T(8,128)(2,1)} async-done(((bf16[2,1024,1,256]{1,3,2,0:T(8,128)(2,1)}), bf16[2,1024,1,256]{1,3,2,0:T(8,128)(2,1)}) %all-reduce.2.cloned.1.call-update) | async-done | bytes 1048592 | tf_op jit(solution)/shard_map/psum | solution.py:111
  77.3 14.4 %fusion.19 = (f32[4,1024]{1,0:T(4,128)S(1)}, f32[4,1024,2048]{2,1,0:T(8,128)}) fusion(pred[1024,2048]{1,0:T(8,128)(4,1)S(1)} %fusion.49, bf16[2,2048,1,256]{1,3,2,0:T(8,128)(2,1)S(1)} %maximum_maximum_fusion, bf16[4,1024,128]{1,2,0:T(8,128)(2,1)S(1)} %copy-done.14, bf16[4,1024,128]{1,2,0:T(8,128)(2,1)S(1)} %copy-done.13), kind=kOutput, calls=%fused_computation.26 | convolution fusion | flops 4324323328 | bytes 38813696 | tf_op jit(solution)/shard_map/kgte,ske->kgts/dot_general | solution.py:61
  91.7 16.4 %fusion.22 = f32[4,1024,256]{2,1,0:T(8,128)} fusion(f32[4,1024,2048]{2,1,0:T(8,128)} %get-tuple-element.313, f32[4,1024]{1,0:T(4,128)S(1)} %get-tuple-element.312, pred[1024,2048]{1,0:T(8,128)(4,1)S(1)} %fusion.49, bf16[2,2048,1,256]{1,3,2,0:T(8,128)(2,1)} %copy-done.8), kind=kOutput, calls=%fused_computation.31 | convolution fusion | flops 4328521728 | bytes 40910848 | tf_op jit(solution)/shard_map/kgts,ske->kgte/dot_general | solution.py:67
  108.1 15.7 %fusion.20 = f32[4,1024]{1,0:T(4,128)S(1)} fusion(f32[4,1024,2048]{2,1,0:T(8,128)} %get-tuple-element.313, f32[4,1024]{1,0:T(4,128)S(1)} %get-tuple-element.312, pred[1024,2048]{1,0:T(8,128)(4,1)S(1)} %fusion.49), kind=kLoop, calls=%fused_computation.27 | loop fusion | flops 33550336 | bytes 35684352 | tf_op jit(solution)/shard_map/reduce_sum | solution.py:66
  126.7 7.8 %fusion.89 = f32[1024,2048]{1,0:T(8,128)} fusion(bf16[2,640,2048]{2,1,0:T(8,128)(2,1)} %param.21, bf16[1024,640]{0,1:T(8,128)(2,1)S(1)} %get-tuple-element.281, f32[640]{0:T(1024)S(1)} %get-tuple-element.254, f32[1024]{0:T(1024)S(1)} %add_rsqrt_fusion.8), kind=kOutput, calls=%fused_computation.133 | convolution fusion | flops 2686976000 | bytes 12327424 | tf_op jit(solution)/shard_map/dot_general | solution.py:53
  134.5 13.5 %fusion.59 = (f32[1024]{0:T(1024)S(1)}, bf16[1024,640]{0,1:T(8,128)(2,1)}) fusion(bf16[2,2048,640]{2,1,0:T(8,128)(2,1)} %param.23, f32[1024,2048]{1,0:T(8,128)} %fusion.89, bf16[2,640,2048]{2,1,0:T(8,128)(2,1)} %param.22, bf16[1024,640]{0,1:T(8,128)(2,1)S(1)} %get-tuple-element.281, f32[640]{0:T(1024)S(1)} %get-tuple-element.254, f32[1024]{0:T(1024)S(1)} %add_rsqrt_fusion.8), kind=kOutput, calls=%fused_computation.102 | convolution fusion | flops 5394922496 | bytes 16263680 | tf_op jit(solution)/shard_map/dot_general | solution.py:56
  179.1 204.1 %while.20 = (s32[]{:T(128)}, bf16[2,1024,1,256]{3,1,2,0:T(8,128)(2,1)S(1)}, f32[1,4,1024]{2,1,0:T(4,128)S(1)}, f32[1,4,1024]{2,1,0:T(4,128)S(1)}, f32[1,4,1024,2...) while((s32[]{:T(128)}, ...), condition=%wide.region_18.0_spmd.clone, body=%wide.region_13.18_spmd.clone.sunk | while | flops 4344264704 | bytes 72642872 | solution.py:124
  182.8 11.7 %collective-permute-done = bf16[2,1024,1,256]{3,1,2,0:T(8,128)(2,1)S(1)} collective-permute-done((bf16[2,1024,1,256]{3,1,2,0:T(8,128)(2,1)S(1)}, bf16[2,1024,1,256]{3,1,2,0:T(8,128)(2,1)S(1)}, u32[]{:S(2)}, u32[]{:S(2)}) %collective-permute-start) | collective-permute-done | bytes 1048608 | tf_op jit(solution)/shard_map/while/body/eval_jaxpr/ppermute | solution.py:119
  194.5 16.3 %conditional.3 = ((f32[1,4,1024]{2,1,0:T(4,128)S(1)}, f32[1,4,1024]{2,1,0:T(4,128)S(1)}, f32[1,4,1024,256]{3,2,1,0:T(8,128)})) conditional(s32[]{:T(128)} %convert_element_type.497, (f32[1,4,1024]{2,1,0:T(4,128)S(1)}, f32[1,4,1024]{2,1,0:T(4,128)S(1)}, f32[1,4,1024,256]{3,2,1,0:T(8,128)}) %tuple.86, (s32[]{:T(128)}, s32[]{:T(128)}, s32[]{:T(128)}, ...), branch_computations={%region_14.14_spmd, %region_15.0_spmd} | conditional | flops 4344264704 | bytes 66347072 | solution.py:121
  203.2 7.6 %bitcast_add_fusion = f32[1,4,1024,256]{3,2,1,0:T(8,128)} fusion(f32[1,4,1024,256]{3,2,1,0:T(8,128)} %get-tuple-element.190, f32[4,1024,1024]{1,2,0:T(8,128)S(1)} %get-tuple-element.283, f32[4,1024]{1,0:T(4,128)S(1)} %bitcast.209, pred[1024,1024]{0,1:T(8,128)(4,1)S(1)} %broadcast_compare_fusion, f32[4,1024]{1,0:T(4,128)S(1)} %get-tuple-element.274, ...), kind=kOutput, calls=%fused_computation.8 | convolution fusion | flops 2166358016 | bytes 26771456 | tf_op jit(solution)/shard_map/while/body/eval_jaxpr/cond/branch_1_fun/kgts,ske->kgte/dot_general | solution.py:79
  210.9 11.7 %collective-permute-done = bf16[2,1024,1,256]{3,1,2,0:T(8,128)(2,1)S(1)} collective-permute-done((bf16[2,1024,1,256]{3,1,2,0:T(8,128)(2,1)S(1)}, bf16[2,1024,1,256]{3,1,2,0:T(8,128)(2,1)S(1)}, u32[]{:S(2)}, u32[]{:S(2)}) %collective-permute-start) | collective-permute-done | bytes 1048608 | tf_op jit(solution)/shard_map/while/body/eval_jaxpr/ppermute | solution.py:119
  222.6 16.3 %conditional.3 = ((f32[1,4,1024]{2,1,0:T(4,128)S(1)}, f32[1,4,1024]{2,1,0:T(4,128)S(1)}, f32[1,4,1024,256]{3,2,1,0:T(8,128)})) conditional(s32[]{:T(128)} %convert_element_type.497, (f32[1,4,1024]{2,1,0:T(4,128)S(1)}, f32[1,4,1024]{2,1,0:T(4,128)S(1)}, f32[1,4,1024,256]{3,2,1,0:T(8,128)}) %tuple.86, (s32[]{:T(128)}, s32[]{:T(128)}, s32[]{:T(128)}, ...), branch_computations={%region_14.14_spmd, %region_15.0_spmd} | conditional | flops 4344264704 | bytes 66347072 | solution.py:121
  239.1 11.7 %collective-permute-done = bf16[2,1024,1,256]{3,1,2,0:T(8,128)(2,1)S(1)} collective-permute-done((bf16[2,1024,1,256]{3,1,2,0:T(8,128)(2,1)S(1)}, bf16[2,1024,1,256]{3,1,2,0:T(8,128)(2,1)S(1)}, u32[]{:S(2)}, u32[]{:S(2)}) %collective-permute-start) | collective-permute-done | bytes 1048608 | tf_op jit(solution)/shard_map/while/body/eval_jaxpr/ppermute | solution.py:119
  250.8 16.3 %conditional.3 = ((f32[1,4,1024]{2,1,0:T(4,128)S(1)}, f32[1,4,1024]{2,1,0:T(4,128)S(1)}, f32[1,4,1024,256]{3,2,1,0:T(8,128)})) conditional(s32[]{:T(128)} %convert_element_type.497, (f32[1,4,1024]{2,1,0:T(4,128)S(1)}, f32[1,4,1024]{2,1,0:T(4,128)S(1)}, f32[1,4,1024,256]{3,2,1,0:T(8,128)}) %tuple.86, (s32[]{:T(128)}, s32[]{:T(128)}, s32[]{:T(128)}, ...), branch_computations={%region_14.14_spmd, %region_15.0_spmd} | conditional | flops 4344264704 | bytes 66347072 | solution.py:121
  259.5 7.6 %bitcast_add_fusion = f32[1,4,1024,256]{3,2,1,0:T(8,128)} fusion(f32[1,4,1024,256]{3,2,1,0:T(8,128)} %get-tuple-element.190, f32[4,1024,1024]{1,2,0:T(8,128)S(1)} %get-tuple-element.283, f32[4,1024]{1,0:T(4,128)S(1)} %bitcast.209, pred[1024,1024]{0,1:T(8,128)(4,1)S(1)} %broadcast_compare_fusion, f32[4,1024]{1,0:T(4,128)S(1)} %get-tuple-element.274, ...), kind=kOutput, calls=%fused_computation.8 | convolution fusion | flops 2166358016 | bytes 26771456 | tf_op jit(solution)/shard_map/while/body/eval_jaxpr/cond/branch_1_fun/kgts,ske->kgte/dot_general | solution.py:79
  267.2 11.7 %collective-permute-done = bf16[2,1024,1,256]{3,1,2,0:T(8,128)(2,1)S(1)} collective-permute-done((bf16[2,1024,1,256]{3,1,2,0:T(8,128)(2,1)S(1)}, bf16[2,1024,1,256]{3,1,2,0:T(8,128)(2,1)S(1)}, u32[]{:S(2)}, u32[]{:S(2)}) %collective-permute-start) | collective-permute-done | bytes 1048608 | tf_op jit(solution)/shard_map/while/body/eval_jaxpr/ppermute | solution.py:119
  278.9 16.3 %conditional.3 = ((f32[1,4,1024]{2,1,0:T(4,128)S(1)}, f32[1,4,1024]{2,1,0:T(4,128)S(1)}, f32[1,4,1024,256]{3,2,1,0:T(8,128)})) conditional(s32[]{:T(128)} %convert_element_type.497, (f32[1,4,1024]{2,1,0:T(4,128)S(1)}, f32[1,4,1024]{2,1,0:T(4,128)S(1)}, f32[1,4,1024,256]{3,2,1,0:T(8,128)}) %tuple.86, (s32[]{:T(128)}, s32[]{:T(128)}, s32[]{:T(128)}, ...), branch_computations={%region_14.14_spmd, %region_15.0_spmd} | conditional | flops 4344264704 | bytes 66347072 | solution.py:121
  295.4 11.7 %collective-permute-done = bf16[2,1024,1,256]{3,1,2,0:T(8,128)(2,1)S(1)} collective-permute-done((bf16[2,1024,1,256]{3,1,2,0:T(8,128)(2,1)S(1)}, bf16[2,1024,1,256]{3,1,2,0:T(8,128)(2,1)S(1)}, u32[]{:S(2)}, u32[]{:S(2)}) %collective-permute-start) | collective-permute-done | bytes 1048608 | tf_op jit(solution)/shard_map/while/body/eval_jaxpr/ppermute | solution.py:119
  307.1 16.3 %conditional.3 = ((f32[1,4,1024]{2,1,0:T(4,128)S(1)}, f32[1,4,1024]{2,1,0:T(4,128)S(1)}, f32[1,4,1024,256]{3,2,1,0:T(8,128)})) conditional(s32[]{:T(128)} %convert_element_type.497, (f32[1,4,1024]{2,1,0:T(4,128)S(1)}, f32[1,4,1024]{2,1,0:T(4,128)S(1)}, f32[1,4,1024,256]{3,2,1,0:T(8,128)}) %tuple.86, (s32[]{:T(128)}, s32[]{:T(128)}, s32[]{:T(128)}, ...), branch_computations={%region_14.14_spmd, %region_15.0_spmd} | conditional | flops 4344264704 | bytes 66347072 | solution.py:121
  323.5 12.7 %collective-permute-done = bf16[2,1024,1,256]{3,1,2,0:T(8,128)(2,1)S(1)} collective-permute-done((bf16[2,1024,1,256]{3,1,2,0:T(8,128)(2,1)S(1)}, bf16[2,1024,1,256]{3,1,2,0:T(8,128)(2,1)S(1)}, u32[]{:S(2)}, u32[]{:S(2)}) %collective-permute-start) | collective-permute-done | bytes 1048608 | tf_op jit(solution)/shard_map/while/body/eval_jaxpr/ppermute | solution.py:119
  336.2 16.3 %conditional.3 = ((f32[1,4,1024]{2,1,0:T(4,128)S(1)}, f32[1,4,1024]{2,1,0:T(4,128)S(1)}, f32[1,4,1024,256]{3,2,1,0:T(8,128)})) conditional(s32[]{:T(128)} %convert_element_type.497, (f32[1,4,1024]{2,1,0:T(4,128)S(1)}, f32[1,4,1024]{2,1,0:T(4,128)S(1)}, f32[1,4,1024,256]{3,2,1,0:T(8,128)}) %tuple.86, (s32[]{:T(128)}, s32[]{:T(128)}, s32[]{:T(128)}, ...), branch_computations={%region_14.14_spmd, %region_15.0_spmd} | conditional | flops 4344264704 | bytes 66347072 | solution.py:121
  352.6 14.2 %collective-permute-done = bf16[2,1024,1,256]{3,1,2,0:T(8,128)(2,1)S(1)} collective-permute-done((bf16[2,1024,1,256]{3,1,2,0:T(8,128)(2,1)S(1)}, bf16[2,1024,1,256]{3,1,2,0:T(8,128)(2,1)S(1)}, u32[]{:S(2)}, u32[]{:S(2)}) %collective-permute-start) | collective-permute-done | bytes 1048608 | tf_op jit(solution)/shard_map/while/body/eval_jaxpr/ppermute | solution.py:119
  366.9 16.3 %conditional.3 = ((f32[1,4,1024]{2,1,0:T(4,128)S(1)}, f32[1,4,1024]{2,1,0:T(4,128)S(1)}, f32[1,4,1024,256]{3,2,1,0:T(8,128)})) conditional(s32[]{:T(128)} %convert_element_type.497, (f32[1,4,1024]{2,1,0:T(4,128)S(1)}, f32[1,4,1024]{2,1,0:T(4,128)S(1)}, f32[1,4,1024,256]{3,2,1,0:T(8,128)}) %tuple.86, (s32[]{:T(128)}, s32[]{:T(128)}, s32[]{:T(128)}, ...), branch_computations={%region_14.14_spmd, %region_15.0_spmd} | conditional | flops 4344264704 | bytes 66347072 | solution.py:121
  394.6 13.5 %fusion.63 = (f32[1024]{0:T(1024)S(1)}, bf16[1024,640]{0,1:T(8,128)(2,1)}) fusion(bf16[2,2048,640]{2,1,0:T(8,128)(2,1)} %param.23, f32[1024,2048]{1,0:T(8,128)} %fusion.84, bf16[2,640,2048]{2,1,0:T(8,128)(2,1)} %param.22, bf16[1024,640]{0,1:T(8,128)(2,1)S(1)} %get-tuple-element.277, f32[640]{0:T(1024)S(1)} %copy-done.19, f32[1024]{0:T(1024)S(1)} %add_rsqrt_fusion.3), kind=kOutput, calls=%fused_computation.106 | convolution fusion | flops 5394922496 | bytes 16263680 | tf_op jit(solution)/shard_map/dot_general | solution.py:56
  (207 shorter events, 199.2 us)
Async XLA Ops:
  7.2 3.6 copy-start.21
  7.2 61.7 %all-reduce.2.cloned.1.call-start = ((), (), s32[]{:S(2)}) async-start(), calls=%async_computation | async-start | bytes 2097152 | tf_op jit(solution)/shard_map/psum | solution.py:111
  11.5 3.4 copy-start.12
  14.7 2.8 copy-start.3
  14.7 2.8 copy-start.4
  17.5 57.7 %collective-permute-start.1 = (bf16[2,1024,1,256]{1,3,2,0:T(8,128)(2,1)}, bf16[2,1024,1,256]{1,3,2,0:T(8,128)(2,1)}, u32[]{:S(2)}, u32[]{:S(2)}) collective-permute-start(bf16[2,1024,1,256]{1,3,2,0:T(8,128)(2,1)} %get-tuple-element.299), channel_id=1, source_target_pairs={{0,1},{1,2},{2,3},{3,4},{4,5},{5,6},{6,7}} | collective-permute-start | bytes 3145736 | tf_op jit(solution)/shard_map/ppermute | solution.py:99
  77.1 14.6 %copy-start.8 = (bf16[2,2048,1,256]{1,3,2,0:T(8,128)(2,1)}, bf16[2,2048,1,256]{1,3,2,0:T(8,128)(2,1)S(1)}, u32[]{:S(2)}) copy-start(bf16[2,2048,1,256]{1,3,2,0:T(8,128)(2,1)S(1)} %maximum_maximum_fusion) | copy-start | bytes 6291460
  108.1 15.7 %copy-start.20 = (bf16[2,4,256,640]{3,2,1,0:T(8,128)(2,1)S(1)}, bf16[2,4,256,640]{3,2,1,0:T(8,128)(2,1)}, u32[]{:S(2)}) copy-start(bf16[2,4,256,640]{3,2,1,0:T(8,128)(2,1)} %param.20) | copy-start | bytes 7864324
  108.1 15.7 %copy-start.25 = (f32[4,1024,256]{2,1,0:T(8,128)S(1)}, f32[4,1024,256]{2,1,0:T(8,128)}, u32[]{:S(2)}) copy-start(f32[4,1024,256]{2,1,0:T(8,128)} %fusion.22) | copy-start | bytes 12582916
  150.1 7.2 %copy-start = (bf16[1024,640]{0,1:T(8,128)(2,1)}, bf16[1024,640]{0,1:T(8,128)(2,1)S(1)}, u32[]{:S(2)}) copy-start(bf16[1024,640]{0,1:T(8,128)(2,1)S(1)} %get-tuple-element.279) | copy-start | bytes 3932164
  151.7 18.7 %copy-start.10 = (bf16[1024,256]{0,1:T(8,128)(2,1)}, bf16[1024,256]{0,1:T(8,128)(2,1)S(1)}, u32[]{:S(2)}) copy-start(bf16[1024,256]{0,1:T(8,128)(2,1)S(1)} %convolution_convert_fusion.2) | copy-start | bytes 1572868
  179.5 15.0 %collective-permute-start = (bf16[2,1024,1,256]{3,1,2,0:T(8,128)(2,1)S(1)}, bf16[2,1024,1,256]{3,1,2,0:T(8,128)(2,1)S(1)}, u32[]{:S(2)}, u32[]{:S(2)}) collective-permute-start(bf16[2,1024,1,256]{3,1,2,0:T(8,128)(2,1)S(1)} %get-tuple-element.399), channel_id=1, source_target_pairs={{0,1},{1,2},{2,3},{3,4},{4,5},{5,6},{6,7},{7,0}} | collective-permute-start | bytes 3145736 | tf_op jit(solution)/shard_map/while/body/eval_jaxpr/ppermute | solution.py:119
  210.9 11.8 %collective-permute-start = (bf16[2,1024,1,256]{3,1,2,0:T(8,128)(2,1)S(1)}, bf16[2,1024,1,256]{3,1,2,0:T(8,128)(2,1)S(1)}, u32[]{:S(2)}, u32[]{:S(2)}) collective-permute-start(bf16[2,1024,1,256]{3,1,2,0:T(8,128)(2,1)S(1)} %get-tuple-element.399), channel_id=1, source_target_pairs={{0,1},{1,2},{2,3},{3,4},{4,5},{5,6},{6,7},{7,0}} | collective-permute-start | bytes 3145736 | tf_op jit(solution)/shard_map/while/body/eval_jaxpr/ppermute | solution.py:119
  239.0 11.8 %collective-permute-start = (bf16[2,1024,1,256]{3,1,2,0:T(8,128)(2,1)S(1)}, bf16[2,1024,1,256]{3,1,2,0:T(8,128)(2,1)S(1)}, u32[]{:S(2)}, u32[]{:S(2)}) collective-permute-start(bf16[2,1024,1,256]{3,1,2,0:T(8,128)(2,1)S(1)} %get-tuple-element.399), channel_id=1, source_target_pairs={{0,1},{1,2},{2,3},{3,4},{4,5},{5,6},{6,7},{7,0}} | collective-permute-start | bytes 3145736 | tf_op jit(solution)/shard_map/while/body/eval_jaxpr/ppermute | solution.py:119
  267.2 11.8 %collective-permute-start = (bf16[2,1024,1,256]{3,1,2,0:T(8,128)(2,1)S(1)}, bf16[2,1024,1,256]{3,1,2,0:T(8,128)(2,1)S(1)}, u32[]{:S(2)}, u32[]{:S(2)}) collective-permute-start(bf16[2,1024,1,256]{3,1,2,0:T(8,128)(2,1)S(1)} %get-tuple-element.399), channel_id=1, source_target_pairs={{0,1},{1,2},{2,3},{3,4},{4,5},{5,6},{6,7},{7,0}} | collective-permute-start | bytes 3145736 | tf_op jit(solution)/shard_map/while/body/eval_jaxpr/ppermute | solution.py:119
  295.3 11.8 %collective-permute-start = (bf16[2,1024,1,256]{3,1,2,0:T(8,128)(2,1)S(1)}, bf16[2,1024,1,256]{3,1,2,0:T(8,128)(2,1)S(1)}, u32[]{:S(2)}, u32[]{:S(2)}) collective-permute-start(bf16[2,1024,1,256]{3,1,2,0:T(8,128)(2,1)S(1)} %get-tuple-element.399), channel_id=1, source_target_pairs={{0,1},{1,2},{2,3},{3,4},{4,5},{5,6},{6,7},{7,0}} | collective-permute-start | bytes 3145736 | tf_op jit(solution)/shard_map/while/body/eval_jaxpr/ppermute | solution.py:119
  323.5 12.7 %collective-permute-start = (bf16[2,1024,1,256]{3,1,2,0:T(8,128)(2,1)S(1)}, bf16[2,1024,1,256]{3,1,2,0:T(8,128)(2,1)S(1)}, u32[]{:S(2)}, u32[]{:S(2)}) collective-permute-start(bf16[2,1024,1,256]{3,1,2,0:T(8,128)(2,1)S(1)} %get-tuple-element.399), channel_id=1, source_target_pairs={{0,1},{1,2},{2,3},{3,4},{4,5},{5,6},{6,7},{7,0}} | collective-permute-start | bytes 3145736 | tf_op jit(solution)/shard_map/while/body/eval_jaxpr/ppermute | solution.py:119
  352.6 14.3 %collective-permute-start = (bf16[2,1024,1,256]{3,1,2,0:T(8,128)(2,1)S(1)}, bf16[2,1024,1,256]{3,1,2,0:T(8,128)(2,1)S(1)}, u32[]{:S(2)}, u32[]{:S(2)}) collective-permute-start(bf16[2,1024,1,256]{3,1,2,0:T(8,128)(2,1)S(1)} %get-tuple-element.399), channel_id=1, source_target_pairs={{0,1},{1,2},{2,3},{3,4},{4,5},{5,6},{6,7},{7,0}} | collective-permute-start | bytes 3145736 | tf_op jit(solution)/shard_map/while/body/eval_jaxpr/ppermute | solution.py:119
  383.2 5.3 %slice-start = ((s8[5242880]{0:T(1024)(128)(4,1)}), s8[4194304]{0:T(1024)(128)(4,1)S(1)}, s32[]{:S(2)}) async-start(s8[5242880]{0:T(1024)(128)(4,1)} %bitcast.224), calls=%async_computation.1 | async-start | bytes 8388608
  383.3 4.5 %copy-start.1 = (bf16[1024,640]{0,1:T(8,128)(2,1)S(1)}, bf16[1024,640]{0,1:T(8,128)(2,1)}, u32[]{:S(2)}) copy-start(bf16[1024,640]{0,1:T(8,128)(2,1)} %copy-done) | copy-start | bytes 3932164
  383.3 4.5 %copy-start.16 = (f32[640]{0:T(1024)S(1)}, f32[640]{0:T(1024)}, u32[]{:S(2)}) copy-start(f32[640]{0:T(1024)} %get-tuple-element.251) | copy-start | bytes 7684
  383.3 5.3 %slice-start.1 = ((s8[5242880]{0:T(1024)(128)(4,1)}), s8[1048576]{0:T(1024)(128)(4,1)S(1)}, s32[]{:S(2)}) async-start(s8[5242880]{0:T(1024)(128)(4,1)} %bitcast.224), calls=%async_computation.2 | async-start | bytes 2097152
  394.5 13.6 %copy-start.17 = (f32[640]{0:T(1024)S(1)}, f32[640]{0:T(1024)}, u32[]{:S(2)}) copy-start(f32[640]{0:T(1024)} %get-tuple-element.250) | copy-start | bytes 7684
  408.1 3.3 copy-start.9
  (13 other events, 19.8 us)
Sparse Core Ops, SparseCore 0:
  19.2 49.5 all-reduce.1
where the time goes:
time: 426 us; the launch traced here: 420 us
  matrix products  180 us (42%)
  waiting for transfers between devices  108 us (25%)
  other arithmetic  81.8 us (19%)
  local copies, waits for them, and re-layouts  29.2 us (7%)
  between operations  15.5 us (4%)
  starting transfers between devices  5.04 us (1%)
    ppermute x7, waiting for transfers between devices, step_fn(): held_kv = lax.ppermute(held_kv, 'cp', perm=shift_perm)  85.5 us
    dot_general x8, matrix products, merge_block(): jnp.einsum('kgts,ske->kgte', exp_scores.astype(jnp.bfloat16), v_blk, pref...  59.4 us
    dot_general x8, matrix products, merge_block(): jnp.einsum('kgte,ske->kgts', q_rot, k_blk, preferred_element_type=jnp.flo...  32.9 us
    reduce_sum x8, other arithmetic, merge_block(): new_sum = decay_fac * run_sum + exp_scores.sum(axis=-1)  29.3 us
    dot_general x2, matrix products, finish(): jnp.dot(hidden, w_down, preferred_element_type=jnp.float32)  27.1 us
    psum x1, waiting for transfers between devices, shard_body(): local_kv = lax.psum(placed, 'cp')  22.8 us
    unnamed x66, local copies, waits for them, and re-layouts  22.2 us
    dot_general x1, matrix products, local_attend(): jnp.einsum('kgts,ske->kgte', exp_scores.astype(jnp.bfloat16), v_win, pref...  16.4 us
  transfers between devices with their start and end apart: 9, of which 8 were waited for; matrix products, arithmetic and copies ran while one was open for 8% of the time, Pallas kernels for 0%

commit v1 on v0

v1 whole, which is shorter than its diff:
```python
import functools

import numpy as np
import jax
import jax.numpy as jnp
from jax import lax
from jax.experimental import pallas as pl
from jax.experimental.pallas import tpu as pltpu
from jax.sharding import PartitionSpec as P

WINDOW = 1024
EPS = 1e-6
BASES = (10000.0, 1000000.0)
SCALES = (1.0, 8.0)
HEAD = 256
TOK = 1024
D = 640
FF = 2048
TILE = 256
LO = 32
LOG2E = 1.4426950408889634
COEF = LOG2E / 16.0
TOP = 36.0
LIMIT = 56.0
NEG = -1e30
F32 = jnp.float32
BF16 = jnp.bfloat16
VLIM = 58 << 20


def rope_const(layer, seq_len):
    base, scale = BASES[layer], SCALES[layer]
    freq = base ** (-np.arange(HEAD // 2, dtype=np.float64) * 2.0 / HEAD)
    hi = (np.arange(seq_len // LO) * LO / scale)[:, None] * freq[None, :]
    lo = (np.arange(LO) / scale)[:, None] * freq[None, :]
    hi_tab = np.concatenate([np.cos(hi), np.sin(hi)], axis=1).astype(np.float32)
    lo_tab = np.concatenate([np.cos(lo), np.sin(lo)], axis=1).astype(np.float32)
    return hi_tab, lo_tab


def rms(x, gain):
    return x * lax.rsqrt(jnp.mean(x * x, axis=-1, keepdims=True) + EPS) * gain


def cos_sin(hi_ref, lo_ref, row0, rows):
    n_hi = rows // LO
    hi = hi_ref[pl.ds(pl.multiple_of(row0 // LO, 8), n_hi), :]
    lo = lo_ref[...]
    ch, sh = hi[:, None, 0:128], hi[:, None, 128:256]
    cl, sl = lo[None, :, 0:128], lo[None, :, 128:256]
    cos = (ch * cl - sh * sl).reshape(rows, 128)
    sin = (sh * cl + ch * sl).reshape(rows, 128)
    return cos, sin


def rotate(x, cos, sin):
    a, b = x[:, 0:128], x[:, 128:256]
    return jnp.concatenate([a * cos - b * sin, b * cos + a * sin], axis=1).astype(BF16)


def head_rope(proj, gain, cos, sin):
    return rotate(rms(proj.astype(BF16).astype(F32), gain), cos, sin)


def dot(a, b):
    return jnp.dot(a, b, preferred_element_type=F32)


def dot_t(a, b):
    return lax.dot_general(a, b, (((1,), (1,)), ((), ())), preferred_element_type=F32)


def qkv_tile(normed, gq, gk, wq, wk, wv, cos, sin, q_ref, kv_ref, k_ref, v_ref):
    k = head_rope(dot(normed, wk[...]), gk, cos, sin)
    v = dot(normed, wv[...]).astype(BF16)
    kv_ref[:, 0:HEAD] = k
    kv_ref[:, HEAD:2 * HEAD] = v
    k_ref[...] = k
    v_ref[...] = v
    for h in range(4):
        q_ref[h] = head_rope(dot(normed, wq[:, h * HEAD:(h + 1) * HEAD]), gq, cos, sin)


def proj_kernel(x_ref, ng_ref, qg_ref, hi_ref, lo_ref, wq_ref, wk_ref, wv_ref, q_ref, kv_ref, k_ref, v_ref):
    i = pl.program_id(0)
    row0 = lax.axis_index('cp') * TOK + i * TILE
    cos, sin = cos_sin(hi_ref, lo_ref, row0, TILE)
    normed = rms(x_ref[...].astype(F32), 1.0 + ng_ref[0:1, :]).astype(BF16)
    qkv_tile(normed, 1.0 + qg_ref[0:1, :], 1.0 + qg_ref[1:2, :], wq_ref, wk_ref, wv_ref, cos, sin, q_ref, kv_ref, k_ref, v_ref)


def whole(shape):
    zeros = (0,) * len(shape)
    return pl.BlockSpec(shape, lambda *_: zeros, pipeline_mode=pl.Buffered(1))


def layer_of(layer, shape):
    idx = (layer,) + (0,) * len(shape)
    return pl.BlockSpec((None,) + shape, lambda *_: idx, pipeline_mode=pl.Buffered(1))


def rows_spec(cols):
    return pl.BlockSpec((TILE, cols), lambda i: (i, 0))


Q_SPEC = pl.BlockSpec((4, TILE, HEAD), lambda i: (0, i, 0))
Q_SHAPE = jax.ShapeDtypeStruct((4, TOK, HEAD), BF16)
KV_SHAPE = jax.ShapeDtypeStruct((TOK, 2 * HEAD), BF16)
K_SHAPE = jax.ShapeDtypeStruct((TOK, HEAD), BF16)
X_SHAPE = jax.ShapeDtypeStruct((TOK, D), BF16)


def project(layer, x, ng, qg, hi, lo, wq, wk, wv):
    return pl.pallas_call(
        proj_kernel,
        grid=(TOK // TILE,),
        in_specs=[rows_spec(D), layer_of(layer, (4, D)), layer_of(layer, (2, HEAD)), whole(hi.shape), whole(lo.shape),
                  layer_of(layer, (D, 4 * HEAD)), layer_of(layer, (D, HEAD)), layer_of(layer, (D, HEAD))],
        out_specs=[Q_SPEC, rows_spec(2 * HEAD), rows_spec(HEAD), rows_spec(HEAD)],
        out_shape=[Q_SHAPE, KV_SHAPE, K_SHAPE, K_SHAPE],
        name=f"project{layer}",
        compiler_params=pltpu.CompilerParams(vmem_limit_bytes=VLIM),
        cost_estimate=pl.CostEstimate(flops=2 * TOK * D * 1536, bytes_accessed=8 << 20, transcendentals=0),
    )(x, ng, qg, hi, lo, wq, wk, wv)


def finish_tile(x, attn, ng, wo, wg, wu, wd):
    o = dot(attn, wo).astype(BF16).astype(F32)
    h1 = (x.astype(F32) + rms(o, 1.0 + ng[1:2, :])).astype(BF16)
    b = rms(h1.astype(F32), 1.0 + ng[2:3, :]).astype(BF16)
    acc = None
    step = 512
    for f in range(0, FF, step):
        g = dot(b, wg[:, f:f + step])
        u = dot(b, wu[:, f:f + step])
        m = (jax.nn.gelu(g, approximate=True) * u).astype(BF16)
        part = dot(m, wd[f:f + step, :])
        acc = part if acc is None else acc + part
    o2 = acc.astype(BF16).astype(F32)
    return (h1.astype(F32) + rms(o2, 1.0 + ng[3:4, :])).astype(BF16)


def local_tile(q_ref, halo_ref, own_ref, win_ref, sigma, fast):
    i = pl.program_id(0)
    first = lax.axis_index('cp') == 0

    @pl.when(i == 0)
    def _():
        win_ref[0:WINDOW, :] = halo_ref[...]
        win_ref[WINDOW:WINDOW + TOK, :] = own_ref[...]

    n_key = WINDOW + TILE
    start = pl.multiple_of(i * TILE, TILE)
    ks = win_ref[pl.ds(start, n_key), 0:HEAD]
    vs = win_ref[pl.ds(start, n_key), HEAD:2 * HEAD]
    col = lax.broadcasted_iota(jnp.int32, (1, n_key), 1)
    hidden = jnp.logical_and(first, col + start < WINDOW)
    r = lax.broadcasted_iota(jnp.int32, (TILE, TILE), 0)
    c = lax.broadcasted_iota(jnp.int32, (TILE, TILE), 1)
    outs = []
    for h in range(4):
        s = dot_t(q_ref[h], ks)
        if fast:
            t = s * COEF + jnp.where(hidden, NEG, -sigma)
        else:
            t = s * COEF + jnp.where(hidden, NEG, 0.0)
        t = jnp.concatenate([jnp.where(c > r, t[:, 0:TILE], NEG), t[:, TILE:WINDOW], jnp.where(c <= r, t[:, WINDOW:], NEG)], axis=1)
        if not fast:
            t = t - jnp.max(t, axis=1, keepdims=True)
        p = jnp.exp2(t)
        total = jnp.sum(p, axis=1, keepdims=True)
        outs.append((dot(p.astype(BF16), vs) / total).astype(BF16))
    return jnp.concatenate(outs, axis=1)


def mid_kernel(fast, sig_ref, q_ref, halo_ref, own_ref, x_ref, ng_ref, ng2_ref, qg_ref, hi_ref, lo_ref,
               wo_hbm, wg_hbm, wu_hbm, wd_hbm, wq_hbm, wk_hbm, wv_hbm,
               mid_ref, q2_ref, kv_ref, k_ref, v_ref,
               win_ref, wo, wg, wu, wd, wq, wk, wv, sems):
    i = pl.program_id(0)
    pairs = [(wo_hbm.at[0], wo), (wg_hbm.at[0], wg), (wu_hbm.at[0], wu), (wd_hbm.at[0], wd),
             (wq_hbm.at[1], wq), (wk_hbm.at[1], wk), (wv_hbm.at[1], wv)]
    copies = [pltpu.make_async_copy(s, d, sems.at[n]) for n, (s, d) in enumerate(pairs)]

    @pl.when(i == 0)
    def _():
        for cp in copies:
            cp.start()

    attn = local_tile(q_ref, halo_ref, own_ref, win_ref, sig_ref[0], fast)

    @pl.when(i == 0)
    def _():
        for cp in copies:
            cp.wait()

    mid = finish_tile(x_ref[...], attn, ng_ref, wo[...], wg, wu, wd)
    mid_ref[...] = mid
    row0 = lax.axis_index('cp') * TOK + i * TILE
    cos, sin = cos_sin(hi_ref, lo_ref, row0, TILE)
    normed = rms(mid.astype(F32), 1.0 + ng2_ref[0:1, :]).astype(BF16)
    qkv_tile(normed, 1.0 + qg_ref[0:1, :], 1.0 + qg_ref[1:2, :], wq, wk, wv, cos, sin, q2_ref, kv_ref, k_ref, v_ref)


ANY = pl.BlockSpec(memory_space=pl.ANY)
SMEM = pl.BlockSpec(memory_space=pltpu.SMEM)
FIN_SCRATCH = [pltpu.VMEM((4 * HEAD, D), BF16), pltpu.VMEM((D, FF), BF16), pltpu.VMEM((D, FF), BF16), pltpu.VMEM((FF, D), BF16)]


def middle(fast, sig, q, halo, own, x, ng, qg, hi, lo, wo, wg, wu, wd, wq, wk, wv):
    return pl.pallas_call(
        functools.partial(mid_kernel, fast),
        grid=(TOK // TILE,),
        in_specs=[SMEM, Q_SPEC, whole((TOK, 2 * HEAD)), whole((TOK, 2 * HEAD)), rows_spec(D), layer_of(0, (4, D)), layer_of(1, (4, D)),
                  layer_of(1, (2, HEAD)), whole(hi.shape), whole(lo.shape)] + [ANY] * 7,
        out_specs=[rows_spec(D), Q_SPEC, rows_spec(2 * HEAD), rows_spec(HEAD), rows_spec(HEAD)],
        out_shape=[X_SHAPE, Q_SHAPE, KV_SHAPE, K_SHAPE, K_SHAPE],
        scratch_shapes=[pltpu.VMEM((WINDOW + TOK, 2 * HEAD), BF16)] + FIN_SCRATCH +
                       [pltpu.VMEM((D, 4 * HEAD), BF16), pltpu.VMEM((D, HEAD), BF16), pltpu.VMEM((D, HEAD), BF16), pltpu.SemaphoreType.DMA((7,))],
        name="middle",
        compiler_params=pltpu.CompilerParams(vmem_limit_bytes=VLIM),
        cost_estimate=pl.CostEstimate(flops=18 * 10**9, bytes_accessed=20 << 20, transcendentals=0),
    )(sig, q, halo, own, x, ng, ng, qg, hi, lo, wo, wg, wu, wd, wq, wk, wv)


def finish_kernel(attn_ref, x_ref, ng_ref, wo_hbm, wg_hbm, wu_hbm, wd_hbm, out_ref, wo, wg, wu, wd, sems):
    i = pl.program_id(0)
    pairs = [(wo_hbm.at[1], wo), (wg_hbm.at[1], wg), (wu_hbm.at[1], wu), (wd_hbm.at[1], wd)]
    copies = [pltpu.make_async_copy(s, d, sems.at[n]) for n, (s, d) in enumerate(pairs)]

    @pl.when(i == 0)
    def _():
        for cp in copies:
            cp.start()
        for cp in copies:
            cp.wait()

    attn = jnp.concatenate([attn_ref[h] for h in range(4)], axis=1)
    out_ref[...] = finish_tile(x_ref[...], attn, ng_ref, wo[...], wg, wu, wd)


def finish(attn, x, ng, wo, wg, wu, wd):
    return pl.pallas_call(
        finish_kernel,
        grid=(TOK // TILE,),
        in_specs=[Q_SPEC, rows_spec(D), layer_of(1, (4, D))] + [ANY] * 4,
        out_specs=rows_spec(D),
        out_shape=X_SHAPE,
        scratch_shapes=FIN_SCRATCH + [pltpu.SemaphoreType.DMA((4,))],
        name="finish",
        compiler_params=pltpu.CompilerParams(vmem_limit_bytes=VLIM),
        cost_estimate=pl.CostEstimate(flops=10 * 10**9, bytes_accessed=12 << 20, transcendentals=0),
    )(attn, x, ng, wo, wg, wu, wd)


def flash_kernel(fast, sig_ref, q_ref, kv_ref, o_ref, acc, l, m):
    me = lax.axis_index('cp')
    i = pl.program_id(0)
    sigma = sig_ref[1]

    def update(ks, vs, width, masked, first):
        if masked:
            r = lax.broadcasted_iota(jnp.int32, (TILE, width), 0) + i * TILE
            vis = lax.broadcasted_iota(jnp.int32, (TILE, width), 1) <= r
        for h in range(4):
            sl = slice(h * TILE, (h + 1) * TILE)
            s = dot_t(q_ref[h], ks)
            if fast:
                t = s * COEF - sigma
                if masked:
                    t = jnp.where(vis, t, NEG)
                p = jnp.exp2(t)
            else:
                t = s * COEF
                if masked:
                    t = jnp.where(vis, t, NEG)
                top = jnp.broadcast_to(jnp.max(t, axis=1, keepdims=True), (TILE, 128))
                new = top if first else jnp.maximum(m[sl], top)
                if not first:
                    decay = jnp.exp2(m[sl] - new)
                    l[sl] = l[sl] * decay
                    acc[sl] = acc[sl] * decay[:, 0:1]
                m[sl] = new
                p = jnp.exp2(t - new[:, 0:1])
            lp = p[:, 0:128]
            for j in range(1, width // 128):
                lp = lp + p[:, j * 128:(j + 1) * 128]
            o = dot(p.astype(BF16), vs)
            if first:
                l[sl] = lp
                acc[sl] = o
            else:
                l[sl] += lp
                acc[sl] += o

    base = pl.multiple_of(me * TOK, TOK)
    update(kv_ref[pl.ds(base, TOK), 0:HEAD], kv_ref[pl.ds(base, TOK), HEAD:2 * HEAD], TOK, True, True)

    def body(j, carry):
        b = pl.multiple_of(j * TOK, TOK)
        update(kv_ref[pl.ds(b, TOK), 0:HEAD], kv_ref[pl.ds(b, TOK), HEAD:2 * HEAD], TOK, False, False)
        return carry

    lax.fori_loop(0, me, body, 0)
    total = jnp.sum(l[...], axis=1, keepdims=True)
    o_ref[...] = (acc[...] / total).astype(BF16).reshape(4, TILE, HEAD)


def flash(fast, sig, q, kv_all):
    return pl.pallas_call(
        functools.partial(flash_kernel, fast),
        grid=(TOK // TILE,),
        in_specs=[SMEM, Q_SPEC, whole(kv_all.shape)],
        out_specs=Q_SPEC,
        out_shape=Q_SHAPE,
        scratch_shapes=[pltpu.VMEM((4 * TILE, HEAD), F32), pltpu.VMEM((4 * TILE, 128), F32), pltpu.VMEM((4 * TILE, 128), F32)],
        name="flash",
        compiler_params=pltpu.CompilerParams(vmem_limit_bytes=VLIM),
        cost_estimate=pl.CostEstimate(flops=32 * 10**9, bytes_accessed=12 << 20, transcendentals=0),
    )(sig, q, kv_all)


def score_bound(qk_gain):
    g = jnp.abs(1.0 + qk_gain)
    pair = jnp.maximum(g[:, 0:HEAD // 2], g[:, HEAD // 2:])
    return 16.0 * 1.02 * jnp.max(pair[0] * pair[1])


def solution(mesh):
    n_dev = mesh.shape['cp']
    rope = [rope_const(layer, TOK * n_dev) for layer in range(2)]
    rounds = [[(7, 5)], [(7, 3), (5, 1)], [(7, 6), (5, 4), (3, 2), (1, 0)]]

    def spread(kv):
        me = lax.axis_index('cp')
        got = kv
        for pairs in rounds:
            new = lax.ppermute(got, 'cp', perm=pairs)
            takes = functools.reduce(jnp.logical_or, [me == r for _, r in pairs])
            got = jnp.where(takes, new, got)
        return got

    def shard_body(x, ng, qg, w_q, w_k, w_v, w_o, w_gate, w_up, w_down):
        wq = w_q.reshape(2, D, 4 * HEAD)
        wk = w_k.reshape(2, D, HEAD)
        wv = w_v.reshape(2, D, HEAD)
        wo = w_o.reshape(2, 4 * HEAD, D)
        bounds = [score_bound(qg[layer]) for layer in range(2)]
        safe = jnp.maximum(bounds[0], bounds[1]) <= LIMIT
        sig = jnp.stack([jnp.maximum(b - TOP, 0.0) * LOG2E for b in bounds])

        def run(fast):
            q, kv, _, _ = project(0, x, ng, qg, *rope[0], wq, wk, wv)
            halo = lax.ppermute(kv, 'cp', perm=[(s, s + 1) for s in range(n_dev - 1)])
            mid, q5, kv5, k5, v5 = middle(fast, sig, q, halo, kv, x, ng, qg, *rope[1], wo, w_gate, w_up, w_down, wq, wk, wv)
            kv_all = lax.all_gather(kv5, 'cp', axis=0, tiled=True)
            last = spread(kv)
            attn = flash(fast, sig, q5, kv_all)
            out = finish(attn, mid, ng, wo, w_gate, w_up, w_down)
            return out, k5, v5, last[:, 0:HEAD], last[:, HEAD:]

        out, k5, v5, kl, vl = lax.cond(safe, lambda: run(True), lambda: run(False))
        return out, k5[:, None, :], v5[:, None, :], kl[:, None, :], vl[:, None, :]

    return jax.shard_map(shard_body, mesh=mesh, in_specs=(P('cp'), P(), P(), P(), P(), P(), P(), P(), P(), P()),
                         out_specs=(P('cp'), P('cp'), P('cp'), P(), P()), check_vma=False)
```

time: 426 us -> 214 us (0.50); the launches traced: 420 us -> 213 us
  matrix products: 180 us -> 0 us
  Pallas kernels: 0 us -> 111 us
  other arithmetic: 81.8 us -> 3.53 us
  waiting for transfers between devices: 108 us -> 57.9 us
  local copies, waits for them, and re-layouts: 29.2 us -> 5.79 us
  starting transfers between devices: 5.04 us -> 18.9 us
    dot_general x30 -> x0, matrix products: 180 us -> none  [the longest x8 59.4 us: merge_block(): jnp.einsum('kgts,ske->kgte', exp_scores.astype(jnp.bfloat16), v_blk, pref...]
    pallas_call x0 -> x4, Pallas kernels: none -> 111 us  [the longest x1 51.6 us: flash(): pl.pallas_call(functools.partial(flash_kernel, fast), grid=(TOK // TILE,)...]
    reduce_sum x13 -> x0, other arithmetic: 48.7 us -> none  [the longest x8 29.3 us: merge_block(): new_sum = decay_fac * run_sum + exp_scores.sum(axis=-1)]
    ppermute x8 -> x4, waiting for transfers between devices: 85.5 us -> 57.9 us  [the longest x3 54.5 us: spread(): new = lax.ppermute(got, 'cp', perm=pairs)]
    psum x1 -> x0, waiting for transfers between devices: 22.8 us -> none  [shard_body(): local_kv = lax.psum(placed, 'cp')]
    unnamed x66 -> x16, local copies, waits for them, and re-layouts: 22.2 us -> 1.4 us
    ppermute x8 -> x4, starting transfers between devices: 5.01 us -> 18.8 us  [the longest x3 17.5 us: spread(): new = lax.ppermute(got, 'cp', perm=pairs)]
    concatenate x6 -> x0, other arithmetic: 9.92 us -> none  [the longest x4 5.4 us: rotate(): jnp.concatenate([lower_half * cos_tab - upper_half * sin_tab, upper_half...]
  transfers between devices with their start and end apart: 9 -> 5, of which waited for: 8 -> 4; matrix products, arithmetic and copies ran while one was open for 8% -> 1% of each run, Pallas kernels for 0% -> 0%
where the time goes in v1:
time: 214 us; the launch traced here: 213 us
  Pallas kernels  111 us (52%)
  waiting for transfers between devices  57.9 us (27%)
  starting transfers between devices  18.9 us (9%)
  between operations  15.4 us (7%)
  local copies, waits for them, and re-layouts  5.79 us (3%)
  other arithmetic  3.53 us (2%)
    ppermute x3, waiting for transfers between devices, spread(): new = lax.ppermute(got, 'cp', perm=pairs)  54.5 us
    pallas_call x1, Pallas kernels, flash(): pl.pallas_call(functools.partial(flash_kernel, fast), grid=(TOK // TILE,)...  51.6 us
    pallas_call x1, Pallas kernels, middle(): pl.pallas_call(functools.partial(mid_kernel, fast), grid=(TOK // TILE,),...  32.5 us
    pallas_call x1, Pallas kernels, finish(): pl.pallas_call(finish_kernel, grid=(TOK // TILE,), in_specs=[Q_SPEC, rows...  20.4 us
    ppermute x3, starting transfers between devices, spread(): new = lax.ppermute(got, 'cp', perm=pairs)  17.5 us
    pallas_call x1, Pallas kernels, project(): pl.pallas_call(proj_kernel, grid=(TOK // TILE,), in_specs=[rows_spec(D),...  6.65 us
    reshape x1, local copies, waits for them, and re-layouts, shard_body(): wq = w_q.reshape(2, D, 4 * HEAD)  4.31 us
  transfers between devices with their start and end apart: 5, of which 4 were waited for; matrix products, arithmetic and copies ran while one was open for 1% of the time, Pallas kernels for 0%

profile of v1, /device:TPU:7, one launch (start us, length us, event | category | flops | bytes accessed | tf_op | source)
XLA Modules:
  0.0 213.3 jit_solution(5563013226006883873)
XLA Ops:
  7.2 0.7 abs_bitcast_fusion
  7.9 0.6 multiply_reduce_fusion.1
  9.1 0.6 multiply_reduce_fusion
  10.4 0.1 pad_maximum_fusion
  10.5 4.3 %reshape.30 = bf16[2,640,1024]{2,1,0:T(8,128)(2,1)S(1)} reshape(bf16[2,640,4,256]{3,2,1,0:T(4,128)(2,1)} %param.19) | data formatting | bytes 5242880 | tf_op jit(solution)/shard_map/reshape | solution.py:344
  14.9 190.2 %conditional.1 = (bf16[1024,640]{1,0:T(8,128)(2,1)S(1)}, bf16[1024,256]{1,0:T(8,128)(2,1)}, bf16[1024,256]{1,0:T(8,128)(2,1)}, bf16[1024,1,256]{2,0,1:T(8,128)(2,1)S(1)}, bf16[1024,1,256]{2,0,1:T(8,128)(2,1)S(1)}) conditional(s32[]{:T(128)} %convert_element_type.3, (bf16[1024,640]{1,0:T(8,128)(2,1)}, f32[2,4,640]{2,1,0:T(4,128)S(1)}, ...), branch_computations={%region_2.3_spmd, %region_3.4_spmd} | conditional | flops 62014836736 | bytes 132120952 | solution.py:362
  15.2 6.7 %project0.3 = (bf16[4,1024,256]{2,1,0:T(8,128)(2,1)}, bf16[1024,512]{1,0:T(8,128)(2,1)}, bf16[1024,256]{1,0:T(8,128)(2,1)}, bf16[1024,256]{1,0:T(8,128)(2,1)}) custom-call(bf16[1024,640]{1,0:T(8,128)(2,1)} %get-tuple-element.85.x_ref, f32[2,4,640]{2,1,0:T(4,128)S(1)} %get-tuple-element.86.ng_ref.ng2_ref, f32[2,2,256]{2,1,0:T(2,128)S(1)} %get-tuple-element.87.qg_ref, ...), custom_call_target="tpu_custom_call" | custom-call | flops 2013265920 | bytes 8388608 | tf_op jit(solution)/shard_map/cond/branch_1_fun/project0/pallas_call | solution.py:114
  21.8 1.3 collective-permute-start.4
  23.1 3.4 %collective-permute-done.4.halo_ref = bf16[1024,512]{1,0:T(8,128)(2,1)} collective-permute-done((bf16[1024,512]{1,0:T(8,128)(2,1)}, bf16[1024,512]{1,0:T(8,128)(2,1)}, u32[]{:S(2)}, u32[]{:S(2)}) %collective-permute-start.4) | collective-permute-done | bytes 1048608 | tf_op jit(solution)/shard_map/cond/branch_1_fun/ppermute | solution.py:354
  26.5 32.5 %middle.3 = (bf16[1024,640]{1,0:T(8,128)(2,1)}, bf16[4,1024,256]{2,1,0:T(8,128)(2,1)}, bf16[1024,512]{1,0:T(8,128)(2,1)}, bf16[1024,256]{1,0:T(8,128)(2,1)}, bf16[1024,256]{1,0:T(8,128)(2,1)}) custom-call(f32[2]{0:T(128)S(1)} %get-tuple-element.84.sig_ref, bf16[4,1024,256]{2,1,0:T(8,128)(2,1)} %get-tuple-element.93.q_ref, ...), custom_call_target="tpu_custom_call" | custom-call | flops 17999998976 | bytes 20971520 | tf_op jit(solution)/shard_map/cond/branch_1_fun/middle/pallas_call | solution.py:211
  59.0 12.9 %collective-permute-start.5 = (bf16[1024,512]{1,0:T(8,128)(2,1)}, bf16[1024,512]{1,0:T(8,128)(2,1)S(1)}, u32[]{:S(2)}, u32[]{:S(2)}) collective-permute-start(bf16[1024,512]{1,0:T(8,128)(2,1)} %get-tuple-element.94.own_ref), channel_id=1, source_target_pairs={{7,5}} | collective-permute-start | bytes 3145736 | tf_op jit(solution)/shard_map/cond/branch_1_fun/ppermute | solution.py:338
  72.0 22.9 %collective-permute-done.5 = bf16[1024,512]{1,0:T(8,128)(2,1)S(1)} collective-permute-done((bf16[1024,512]{1,0:T(8,128)(2,1)}, bf16[1024,512]{1,0:T(8,128)(2,1)S(1)}, u32[]{:S(2)}, u32[]{:S(2)}) %collective-permute-start.5) | collective-permute-done | bytes 1048608 | tf_op jit(solution)/shard_map/cond/branch_1_fun/ppermute | solution.py:338
  94.9 1.3 broadcast_select_fusion.3
  96.2 2.3 %collective-permute-start.6 = (bf16[1024,512]{1,0:T(8,128)(2,1)S(1)}, bf16[1024,512]{1,0:T(8,128)(2,1)}, u32[]{:S(2)}, u32[]{:S(2)}) collective-permute-start(bf16[1024,512]{1,0:T(8,128)(2,1)S(1)} %broadcast_select_fusion.3), channel_id=1, source_target_pairs={{7,3},{5,1}} | collective-permute-start | bytes 3145736 | tf_op jit(solution)/shard_map/cond/branch_1_fun/ppermute | solution.py:338
  98.5 30.4 %collective-permute-done.6 = bf16[1024,512]{1,0:T(8,128)(2,1)} collective-permute-done((bf16[1024,512]{1,0:T(8,128)(2,1)S(1)}, bf16[1024,512]{1,0:T(8,128)(2,1)}, u32[]{:S(2)}, u32[]{:S(2)}) %collective-permute-start.6) | collective-permute-done | bytes 1048608 | tf_op jit(solution)/shard_map/cond/branch_1_fun/ppermute | solution.py:338
  128.9 0.1 broadcast_select_fusion.4
  129.0 2.3 %collective-permute-start.7 = (bf16[1024,512]{1,0:T(8,128)(2,1)S(1)}, bf16[1024,512]{1,0:T(8,128)(2,1)}, u32[]{:S(2)}, u32[]{:S(2)}) collective-permute-start(bf16[1024,512]{1,0:T(8,128)(2,1)S(1)} %broadcast_select_fusion.4), channel_id=1, source_target_pairs={{7,6},{5,4},{3,2},{1,0}} | collective-permute-start | bytes 3145736 | tf_op jit(solution)/shard_map/cond/branch_1_fun/ppermute | solution.py:338
  131.3 1.3 collective-permute-done.7
  132.5 0.1 broadcast_select_fusion.5
  132.8 51.6 %flash.3.attn_ref = bf16[4,1024,256]{2,1,0:T(8,128)(2,1)} custom-call(f32[2]{0:T(128)S(1)} %get-tuple-element.84.sig_ref, bf16[4,1024,256]{2,1,0:T(8,128)(2,1)} %get-tuple-element.101.q_ref, bf16[8192,512]{1,0:T(8,128)(2,1)} %all-gather.5.cloned.1.call-done.kv_ref), custom_call_target="tpu_custom_call" | custom-call | flops 32000000000 | bytes 12582912 | tf_op jit(solution)/shard_map/cond/branch_1_fun/flash/pallas_call | solution.py:310
  184.3 20.4 %finish.3 = bf16[1024,640]{1,0:T(8,128)(2,1)S(1)} custom-call(bf16[4,1024,256]{2,1,0:T(8,128)(2,1)} %flash.3.attn_ref, bf16[1024,640]{1,0:T(8,128)(2,1)} %get-tuple-element.103.x_ref, f32[2,4,640]{2,1,0:T(4,128)S(1)} %get-tuple-element.86.ng_ref.ng2_ref, bf16[2,1024,640]{2,1,0:T(8,128)(2,1)S(1)} %copy-done.6, ...), custom_call_target="tpu_custom_call" | custom-call | flops 10000000000 | bytes 12582912 | tf_op jit(solution)/shard_map/cond/branch_1_fun/finish/pallas_call | solution.py:243
  205.1 0.8 copy-done
  205.9 0.2 copy-done.1
  206.0 0.4 copy-done.9
  (22 shorter events, 0.2 us)
Async XLA Ops:
  10.5 4.3 %copy-start.2 = (f32[2,2,256]{2,1,0:T(2,128)S(1)}, f32[2,2,256]{2,1,0:T(2,128)}, u32[]{:S(2)}) copy-start(f32[2,2,256]{2,1,0:T(2,128)} %param.18) | copy-start | bytes 12292
  10.5 4.3 %copy-start.7 = (bf16[2,640,1,256]{3,1,2,0:T(8,128)(2,1)S(1)}, bf16[2,640,1,256]{3,1,2,0:T(8,128)(2,1)}, u32[]{:S(2)}) copy-start(bf16[2,640,1,256]{3,1,2,0:T(8,128)(2,1)} %param.20) | copy-start | bytes 1966084
  10.5 4.4 %copy-start.8 = (f32[2,4,640]{2,1,0:T(4,128)S(1)}, f32[2,4,640]{2,1,0:T(4,128)}, u32[]{:S(2)}) copy-start(f32[2,4,640]{2,1,0:T(4,128)} %param.17) | copy-start | bytes 61444
  10.5 4.4 %copy-start.10 = (f32[32,256]{1,0:T(8,128)S(1)}, f32[32,256]{1,0:T(8,128)}, u32[]{:S(2)}) copy-start(f32[32,256]{1,0:T(8,128)} %constant.63.clone) | copy-start | bytes 98308
  10.5 4.4 %copy-start.11 = (f32[32,256]{1,0:T(8,128)S(1)}, f32[32,256]{1,0:T(8,128)}, u32[]{:S(2)}) copy-start(f32[32,256]{1,0:T(8,128)} %constant.61.clone) | copy-start | bytes 98308
  15.1 117.7 %all-gather.5.cloned.1.call-start = ((), (), s32[]{:S(2)}) async-start(), calls=%async_computation.1 | async-start | bytes 9437184 | tf_op jit(solution)/shard_map/cond/branch_1_fun/all_gather | solution.py:356
  15.2 11.3 %copy-start.5 = (bf16[2,1024,640]{2,1,0:T(8,128)(2,1)S(1)}, bf16[2,1024,640]{2,1,0:T(8,128)(2,1)}, u32[]{:S(2)}) copy-start(bf16[2,1024,640]{2,1,0:T(8,128)(2,1)} %get-tuple-element.97.wo_hbm) | copy-start | bytes 7864324 | tf_op jit(solution)/shard_map/cond
  21.8 4.7 %collective-permute-start.4 = (bf16[1024,512]{1,0:T(8,128)(2,1)}, bf16[1024,512]{1,0:T(8,128)(2,1)}, u32[]{:S(2)}, u32[]{:S(2)}) collective-permute-start(bf16[1024,512]{1,0:T(8,128)(2,1)} %get-tuple-element.94.own_ref), channel_id=1, source_target_pairs={{0,1},{1,2},{2,3},{3,4},{4,5},{5,6},{6,7}} | collective-permute-start | bytes 3145736 | tf_op jit(solution)/shard_map/cond/branch_1_fun/ppermute | solution.py:354
  59.0 35.8 %collective-permute-start.5 = (bf16[1024,512]{1,0:T(8,128)(2,1)}, bf16[1024,512]{1,0:T(8,128)(2,1)S(1)}, u32[]{:S(2)}, u32[]{:S(2)}) collective-permute-start(bf16[1024,512]{1,0:T(8,128)(2,1)} %get-tuple-element.94.own_ref), channel_id=1, source_target_pairs={{7,5}} | collective-permute-start | bytes 3145736 | tf_op jit(solution)/shard_map/cond/branch_1_fun/ppermute | solution.py:338
  96.2 32.7 %collective-permute-start.6 = (bf16[1024,512]{1,0:T(8,128)(2,1)S(1)}, bf16[1024,512]{1,0:T(8,128)(2,1)}, u32[]{:S(2)}, u32[]{:S(2)}) collective-permute-start(bf16[1024,512]{1,0:T(8,128)(2,1)S(1)} %broadcast_select_fusion.3), channel_id=1, source_target_pairs={{7,3},{5,1}} | collective-permute-start | bytes 3145736 | tf_op jit(solution)/shard_map/cond/branch_1_fun/ppermute | solution.py:338
  129.0 3.6 %collective-permute-start.7 = (bf16[1024,512]{1,0:T(8,128)(2,1)S(1)}, bf16[1024,512]{1,0:T(8,128)(2,1)}, u32[]{:S(2)}, u32[]{:S(2)}) collective-permute-start(bf16[1024,512]{1,0:T(8,128)(2,1)S(1)} %broadcast_select_fusion.4), channel_id=1, source_target_pairs={{7,6},{5,4},{3,2},{1,0}} | collective-permute-start | bytes 3145736 | tf_op jit(solution)/shard_map/cond/branch_1_fun/ppermute | solution.py:338
  132.8 51.6 %copy-start.6 = (bf16[2,1024,640]{2,1,0:T(8,128)(2,1)S(1)}, bf16[2,1024,640]{2,1,0:T(8,128)(2,1)}, u32[]{:S(2)}) copy-start(bf16[2,1024,640]{2,1,0:T(8,128)(2,1)} %get-tuple-element.97.wo_hbm) | copy-start | bytes 7864324 | tf_op jit(solution)/shard_map/cond
  205.1 0.8 copy-start
  205.1 1.0 copy-start.1
  205.1 1.4 copy-start.9
Sparse Core Ops, SparseCore 0:
  59.1 72.3 all-gather.4

commit v2 on v0

v2 whole, which is shorter than its diff:
```python
import functools

import numpy as np
import jax
import jax.numpy as jnp
from jax import lax
from jax.experimental import pallas as pl
from jax.experimental.pallas import tpu as pltpu
from jax.sharding import PartitionSpec as P

WINDOW = 1024
EPS = 1e-6
BASES = (10000.0, 1000000.0)
SCALES = (1.0, 8.0)
HEAD = 256
TOK = 1024
D = 640
FF = 2048
TILE = 256
LO = 32
LOG2E = 1.4426950408889634
COEF = LOG2E / 16.0
TOP = 36.0
LIMIT = 56.0
NEG = -1e30
F32 = jnp.float32
BF16 = jnp.bfloat16
VLIM = 58 << 20


def rope_const(layer, seq_len):
    base, scale = BASES[layer], SCALES[layer]
    freq = base ** (-np.arange(HEAD // 2, dtype=np.float64) * 2.0 / HEAD)
    hi = (np.arange(seq_len // LO) * LO / scale)[:, None] * freq[None, :]
    lo = (np.arange(LO) / scale)[:, None] * freq[None, :]
    hi_tab = np.concatenate([np.cos(hi), np.sin(hi)], axis=1).astype(np.float32)
    lo_tab = np.concatenate([np.cos(lo), np.sin(lo)], axis=1).astype(np.float32)
    return hi_tab, lo_tab


def rms(x, gain):
    return x * lax.rsqrt(jnp.mean(x * x, axis=-1, keepdims=True) + EPS) * gain


def cos_sin(hi_ref, lo_ref, row0, rows):
    n_hi = rows // LO
    hi = hi_ref[pl.ds(pl.multiple_of(row0 // LO, 8), n_hi), :]
    lo = lo_ref[...]
    ch, sh = hi[:, None, 0:128], hi[:, None, 128:256]
    cl, sl = lo[None, :, 0:128], lo[None, :, 128:256]
    cos = (ch * cl - sh * sl).reshape(rows, 128)
    sin = (sh * cl + ch * sl).reshape(rows, 128)
    return cos, sin


def rotate(x, cos, sin):
    a, b = x[:, 0:128], x[:, 128:256]
    return jnp.concatenate([a * cos - b * sin, b * cos + a * sin], axis=1).astype(BF16)


def head_rope(proj, gain, cos, sin):
    return rotate(rms(proj.astype(BF16).astype(F32), gain), cos, sin)


def dot(a, b):
    return jnp.dot(a, b, preferred_element_type=F32)


def dot_t(a, b):
    return lax.dot_general(a, b, (((1,), (1,)), ((), ())), preferred_element_type=F32)


MESH = pl.DeviceIdType.MESH
N_SLOT = 7
N_TILE = TOK // TILE
QROWS = 512
FROWS = 512
FSTEP = 512


def finish_rows(x, attn, ng, wo, wg, wu, wd):
    o = dot(attn, wo[...]).astype(BF16).astype(F32)
    h1 = (x.astype(F32) + rms(o, 1.0 + ng[1:2, :])).astype(BF16)
    b = rms(h1.astype(F32), 1.0 + ng[2:3, :]).astype(BF16)
    acc = None
    for f in range(0, FF, FSTEP):
        g = dot(b, wg[:, f:f + FSTEP])
        u = dot(b, wu[:, f:f + FSTEP])
        m = (jax.nn.gelu(g, approximate=True) * u).astype(BF16)
        part = dot(m, wd[f:f + FSTEP, :])
        acc = part if acc is None else acc + part
    o2 = acc.astype(BF16).astype(F32)
    return (h1.astype(F32) + rms(o2, 1.0 + ng[3:4, :])).astype(BF16)


def layers_kernel(fast, sig_ref, ng_ref, qg_ref, hi4_ref, lo4_ref, hi5_ref, lo5_ref, x_hbm, wq_hbm, wk_hbm, wv_hbm, wo_hbm, wg_hbm, wu_hbm, wd_hbm,
                  out_hbm, k_hbm, v_hbm, kl_hbm, vl_hbm,
                  x, mid, win, kv5, q, buf, acc, l, m, last, xo, wq, wk, wv, wo, wg, wu, wd,
                  load_sem, out_sem, halo_send, halo_recv, hop_send, hop_recv, pass_send, over_send, wide_recv, last_send, last_recv):
    me = lax.axis_index('cp')
    core = me % 2
    chip = me // 2
    partner = me + 1 - 2 * core
    xnb = me + 2 - 4 * (chip % 2)
    ynb = me + 4 - 8 * (chip // 2)
    top = 7
    is_last = me == top

    def load(src, dst, n):
        return pltpu.make_async_copy(src, dst, load_sem.at[n])

    early = [load(x_hbm, x, 0), load(wk_hbm.at[0], wk.at[0], 1), load(wv_hbm.at[0], wv.at[0], 2), load(wq_hbm.at[0], wq.at[0], 3)]
    ff4 = [load(wo_hbm.at[0], wo, 4), load(wg_hbm.at[0], wg, 5), load(wu_hbm.at[0], wu, 6), load(wd_hbm.at[0], wd, 7)]
    next_qkv = [load(wk_hbm.at[1], wk.at[1], 8), load(wv_hbm.at[1], wv.at[1], 9), load(wq_hbm.at[1], wq.at[1], 10)]
    ff5 = [load(wo_hbm.at[1], wo, 4), load(wg_hbm.at[1], wg, 5), load(wu_hbm.at[1], wu, 6), load(wd_hbm.at[1], wd, 7)]
    for cp in early:
        cp.start()

    if fast:
        barrier = pltpu.get_barrier_semaphore()
        for other in (partner, xnb, ynb, (me + 1) % 8, (me + 7) % 8):
            pl.semaphore_signal(barrier, inc=1, device_id=(other,), device_id_type=MESH)
    for cp in ff4 + next_qkv:
        cp.start()

    @pl.when(me == 0)
    def _():
        win[0:WINDOW, :] = jnp.zeros((WINDOW, 2 * HEAD), BF16)

    if fast:
        pl.semaphore_wait(barrier, 5)

    def send(src, dst, ssem, rsem, dev):
        return pltpu.make_async_remote_copy(src_ref=src, dst_ref=dst, send_sem=ssem, recv_sem=rsem, device_id=(dev,), device_id_type=MESH)

    def on(cond, copy, act):
        @pl.when(cond)
        def _():
            getattr(copy, act)()

    def rows_of(t, n=TILE):
        return pl.ds(pl.multiple_of(t * n, n), n)

    def halo_copy(t):
        return send(win.at[rows_of(t + N_TILE)], win.at[rows_of(t)], halo_send.at[t], halo_recv.at[t], (me + 1) % 8)

    g4q, g4k = 1.0 + qg_ref[0, 0:1, :], 1.0 + qg_ref[0, 1:2, :]
    g5q, g5k = 1.0 + qg_ref[1, 0:1, :], 1.0 + qg_ref[1, 1:2, :]
    for cp in early[:3]:
        cp.wait()

    def kv_tile(it, carry):
        t = N_TILE - 1 - it
        cos, sin = cos_sin(hi4_ref, lo4_ref, me * TOK + t * TILE, TILE)
        a = rms(x[rows_of(t), :].astype(F32), 1.0 + ng_ref[0, 0:1, :]).astype(BF16)
        win[rows_of(t + N_TILE), 0:HEAD] = head_rope(dot(a, wk[0]), g4k, cos, sin)
        win[rows_of(t + N_TILE), HEAD:2 * HEAD] = dot(a, wv[0]).astype(BF16)
        on(me < top, halo_copy(t), 'start')
        return carry

    lax.fori_loop(0, N_TILE, kv_tile, 0)
    own4 = win.at[pl.ds(WINDOW, TOK)]
    last_cps = [send(own4, last, last_send.at[n], last_recv, dev) for n, dev in enumerate((partner, xnb, ynb))]
    for cp in last_cps:
        on(is_last, cp, 'start')
    early[3].wait()
    for cp in ff4 + next_qkv:
        cp.wait()

    def hops(t):
        def hop(k, slot, rk, dev):
            return send(kv5.at[rows_of(t)], buf.at[slot, rows_of(t)], hop_send.at[k, t], hop_recv.at[rk, t], dev)
        return [(core == 0, hop(0, 0, 0, partner)),
                (chip == 0, hop(1, 1, 1, xnb)),
                (chip == 0, hop(2, 1, 1, ynb)),
                (chip == 1, hop(2, 1, 1, ynb)),
                (chip == 2, hop(1, 3, 2, xnb))]

    sig4, sig5 = sig_ref[0], sig_ref[1]
    n_key = WINDOW + TILE

    def layer_tile(it, carry):
        t = N_TILE - 1 - it
        rows = rows_of(t)
        cos, sin = cos_sin(hi4_ref, lo4_ref, me * TOK + t * TILE, TILE)
        a = rms(x[rows, :].astype(F32), 1.0 + ng_ref[0, 0:1, :]).astype(BF16)
        qs = [head_rope(dot(a, wq[0, :, h * HEAD:(h + 1) * HEAD]), g4q, cos, sin) for h in range(4)]

        on(me > 0, halo_copy(t), 'wait_recv')
        start = pl.multiple_of(t * TILE, TILE)
        ks = win[pl.ds(start, n_key), 0:HEAD]
        vs = win[pl.ds(start, n_key), HEAD:2 * HEAD]
        col = lax.broadcasted_iota(jnp.int32, (1, n_key), 1)
        hidden = jnp.logical_and(me == 0, col + start < WINDOW)
        bias = jnp.where(hidden, NEG, -sig4 if fast else 0.0)
        r = lax.broadcasted_iota(jnp.int32, (TILE, TILE), 0)
        c = lax.broadcasted_iota(jnp.int32, (TILE, TILE), 1)
        outs = []
        for h in range(4):
            s = dot_t(qs[h], ks) * COEF + bias
            s = jnp.concatenate([jnp.where(c > r, s[:, 0:TILE], NEG), s[:, TILE:WINDOW], jnp.where(c <= r, s[:, WINDOW:], NEG)], axis=1)
            if not fast:
                s = s - jnp.max(s, axis=1, keepdims=True)
            p = jnp.exp2(s)
            total = jnp.sum(p, axis=1, keepdims=True)
            outs.append((dot(p.astype(BF16), vs) / total).astype(BF16))
        h_mid = finish_rows(x[rows, :], jnp.concatenate(outs, axis=1), ng_ref[0], wo, wg, wu, wd)
        mid[rows, :] = h_mid
        cos, sin = cos_sin(hi5_ref, lo5_ref, me * TOK + t * TILE, TILE)
        a = rms(h_mid.astype(F32), 1.0 + ng_ref[1, 0:1, :]).astype(BF16)
        kv5[rows, 0:HEAD] = head_rope(dot(a, wk[1]), g5k, cos, sin)
        kv5[rows, HEAD:2 * HEAD] = dot(a, wv[1]).astype(BF16)
        for h in range(4):
            q[h, rows, :] = head_rope(dot(a, wq[1, :, h * HEAD:(h + 1) * HEAD]), g5q, cos, sin)
        for cond, cp in hops(t):
            on(cond, cp, 'start')
        return carry

    lax.fori_loop(0, N_TILE, layer_tile, 0)
    outs5 = [pltpu.make_async_copy(kv5.at[:, pl.ds(0, HEAD)], k_hbm, out_sem.at[0]), pltpu.make_async_copy(kv5.at[:, pl.ds(HEAD, HEAD)], v_hbm, out_sem.at[1])]
    for cp in outs5 + ff5:
        cp.start()

    def attend(ks, vs, rows, width, masked, first):
        n = rows.size
        if masked:
            r = lax.broadcasted_iota(jnp.int32, (n, n), 0)
            vis = lax.broadcasted_iota(jnp.int32, (n, n), 1) <= r
        for h in range(4):
            s = dot_t(q[h, rows, :], ks)
            t = s * COEF - sig5 if fast else s * COEF
            if masked:
                tail = jnp.where(vis, t[:, width - n:], NEG)
                t = tail if width == n else jnp.concatenate([t[:, 0:width - n], tail], axis=1)
            if not fast:
                mx = jnp.broadcast_to(jnp.max(t, axis=1, keepdims=True), (n, 128))
                fresh = mx if first else jnp.maximum(m[h, rows, :], mx)
                if not first:
                    decay = jnp.exp2(m[h, rows, :] - fresh)
                    l[h, rows, :] = l[h, rows, :] * decay
                    acc[h, rows, :] = acc[h, rows, :] * decay[:, 0:1]
                m[h, rows, :] = fresh
                t = t - fresh[:, 0:1]
            p = jnp.exp2(t)
            lp = p[:, 0:128]
            for j in range(1, width // 128):
                lp = lp + p[:, j * 128:(j + 1) * 128]
            o = dot(p.astype(BF16), vs)
            if first:
                l[h, rows, :] = lp
                acc[h, rows, :] = o
            else:
                l[h, rows, :] += lp
                acc[h, rows, :] += o

    for i in range(N_TILE):
        width = (i + 1) * TILE
        attend(kv5[0:width, 0:HEAD], kv5[0:width, HEAD:2 * HEAD], pl.ds(i * TILE, TILE), width, True, True)

    def slot(s):
        ks = buf[s, :, 0:HEAD]
        vs = buf[s, :, HEAD:2 * HEAD]

        def q_rows(i, carry):
            attend(ks, vs, rows_of(i, QROWS), TOK, False, False)
            return carry

        lax.fori_loop(0, TOK // QROWS, q_rows, 0)

    def wide(s, dst, ssem, dev):
        return send(buf.at[s], buf.at[dst], ssem, wide_recv.at[dst], dev)

    def relay(s):
        odd = s % 2 == 1
        return [(odd, wide(s, jnp.minimum(s + 1, N_SLOT - 1), pass_send.at[s], partner)),
                (jnp.logical_and(chip == 3, s == 1), wide(s, 3, over_send, xnb)),
                (jnp.logical_and(jnp.logical_and(chip == 1, core == 0), s == 1), wide(s, 5, over_send, ynb)),
                (jnp.logical_and(jnp.logical_and(chip == 2, core == 1), s == 1), wide(s, 5, over_send, xnb))]

    def chunks_in(cond, slot_no, rk):
        @pl.when(cond)
        def _():
            def one(t, carry):
                send(kv5.at[rows_of(t)], buf.at[slot_no, rows_of(t)], hop_send.at[0, t], hop_recv.at[rk, t], partner).wait_recv()
                return carry
            lax.fori_loop(0, N_TILE, one, 0)

    gives = jnp.logical_or(me == 3, jnp.logical_or(me == 5, me == 1))
    spread = [(gives, send(last, last, last_send.at[0], last_recv, partner)), (me == 3, send(last, last, last_send.at[1], last_recv, xnb))]

    def pass_last(cond):
        @pl.when(cond)
        def _():
            send(last, last, last_send.at[2], last_recv, partner).wait_recv()
            for c, cp in spread:
                on(c, cp, 'start')

    pass_last(jnp.logical_and(gives, me > 1))

    def step(s, carry):
        chunks_in(jnp.logical_and(s == 0, core == 1), 0, 0)
        chunks_in(s == 1, 1, 1)
        chunks_in(jnp.logical_and(s == 3, chip == 3), 3, 2)

        @pl.when(jnp.logical_or(jnp.logical_and(s > 0, s % 2 == 0), jnp.logical_or(s == 5, jnp.logical_and(s == 3, chip == 2))))
        def _():
            wide(s, s, pass_send.at[s], partner).wait_recv()

        for cond, cp in relay(s):
            on(cond, cp, 'start')

        @pl.when(jnp.logical_or(s >= 1, core == 1))
        def _():
            slot(s)

        return carry

    lax.fori_loop(0, 2 * chip + 1, step, 0)
    pass_last(me == 1)

    @pl.when(jnp.logical_and(jnp.logical_not(gives), jnp.logical_not(is_last)))
    def _():
        send(last, last, last_send.at[2], last_recv, partner).wait_recv()

    def put_last(src):
        return [pltpu.make_async_copy(src.at[:, pl.ds(0, HEAD)], kl_hbm, out_sem.at[2]), pltpu.make_async_copy(src.at[:, pl.ds(HEAD, HEAD)], vl_hbm, out_sem.at[3])]

    for cp in put_last(own4):
        on(is_last, cp, 'start')
    for cp in put_last(last):
        on(jnp.logical_not(is_last), cp, 'start')

    for cp in ff5:
        cp.wait()

    def out_copy(t):
        return pltpu.make_async_copy(xo.at[rows_of(t, FROWS)], out_hbm.at[rows_of(t, FROWS)], out_sem.at[4 + t])

    def finish_tile(t, carry):
        rows = rows_of(t, FROWS)
        attn = []
        for h in range(4):
            total = jnp.sum(l[h, rows, :], axis=1, keepdims=True)
            attn.append((acc[h, rows, :] / total).astype(BF16))
        xo[rows, :] = finish_rows(mid[rows, :], jnp.concatenate(attn, axis=1), ng_ref[1], wo, wg, wu, wd)
        out_copy(t).start()
        return carry

    lax.fori_loop(0, TOK // FROWS, finish_tile, 0)

    def drain_tile(t, carry):
        on(me < top, halo_copy(t), 'wait_send')
        for cond, cp in hops(t):
            on(cond, cp, 'wait_send')
        return carry

    lax.fori_loop(0, N_TILE, drain_tile, 0)

    def drain_step(s, carry):
        for cond, cp in relay(s):
            on(cond, cp, 'wait_send')
        return carry

    lax.fori_loop(1, 2 * chip + 1, drain_step, 0)
    for cp in last_cps:
        on(is_last, cp, 'wait_send')
    for cond, cp in spread:
        on(cond, cp, 'wait_send')
    for cp in outs5 + put_last(last):
        cp.wait()
    for t in range(TOK // FROWS):
        out_copy(t).wait()


def layers(fast, sig, ng, qg, rope, x, wq, wk, wv, wo, wg, wu, wd):
    vm = pl.BlockSpec(memory_space=pltpu.VMEM)
    anyw = pl.BlockSpec(memory_space=pl.ANY)
    dma = pltpu.SemaphoreType.DMA
    kshape = jax.ShapeDtypeStruct((TOK, HEAD), BF16)
    return pl.pallas_call(
        functools.partial(layers_kernel, fast),
        in_specs=[pl.BlockSpec(memory_space=pltpu.SMEM)] + [vm] * 6 + [anyw] * 8,
        out_specs=[anyw] * 5,
        out_shape=[jax.ShapeDtypeStruct((TOK, D), BF16), kshape, kshape, kshape, kshape],
        scratch_shapes=[
            pltpu.VMEM((TOK, D), BF16), pltpu.VMEM((TOK, D), BF16), pltpu.VMEM((WINDOW + TOK, 2 * HEAD), BF16), pltpu.VMEM((TOK, 2 * HEAD), BF16),
            pltpu.VMEM((4, TOK, HEAD), BF16), pltpu.VMEM((N_SLOT, TOK, 2 * HEAD), BF16), pltpu.VMEM((4, TOK, HEAD), F32), pltpu.VMEM((4, TOK, 128), F32),
            pltpu.VMEM((8, 128) if fast else (4, TOK, 128), F32), pltpu.VMEM((TOK, 2 * HEAD), BF16), pltpu.VMEM((TOK, D), BF16),
            pltpu.VMEM((2, D, 4 * HEAD), BF16), pltpu.VMEM((2, D, HEAD), BF16), pltpu.VMEM((2, D, HEAD), BF16),
            pltpu.VMEM((4 * HEAD, D), BF16), pltpu.VMEM((D, FF), BF16), pltpu.VMEM((D, FF), BF16), pltpu.VMEM((FF, D), BF16),
            dma((11,)), dma((4 + TOK // FROWS,)), dma((N_TILE,)), dma((N_TILE,)), dma((3, N_TILE)), dma((3, N_TILE)), dma((N_SLOT,)), dma, dma((N_SLOT,)),
            dma((3,)), dma],
        name="layers_fast" if fast else "layers_safe",
        compiler_params=pltpu.CompilerParams(vmem_limit_bytes=VLIM, collective_id=0 if fast else None, has_side_effects=True),
        cost_estimate=pl.CostEstimate(flops=60 * 10**9, bytes_accessed=30 << 20, transcendentals=0),
    )(sig, ng, qg, *rope[0], *rope[1], x, wq, wk, wv, wo, wg, wu, wd)


def score_bound(qk_gains):
    g = jnp.abs(1.0 + qk_gains)
    pair = jnp.maximum(g[:, :, 0:HEAD // 2], g[:, :, HEAD // 2:])
    return 16.0 * 1.02 * jnp.max(pair[:, 0] * pair[:, 1])


def solution(mesh):
    n_dev = mesh.shape['cp']
    rope = [rope_const(layer, TOK * n_dev) for layer in range(2)]

    def shard_body(x, ng, qg, w_q, w_k, w_v, w_o, w_gate, w_up, w_down):
        wq = w_q.reshape(2, D, 4 * HEAD)
        wk = w_k.reshape(2, D, HEAD)
        wv = w_v.reshape(2, D, HEAD)
        wo = w_o.reshape(2, 4 * HEAD, D)
        bound = score_bound(qg)
        safe = bound <= LIMIT
        sig = jnp.full((2,), jnp.maximum(bound - TOP, 0.0) * LOG2E)

        def run(fast):
            return tuple(layers(fast, sig, ng, qg, rope, x, wq, wk, wv, wo, w_gate, w_up, w_down))

        start = (jnp.logical_not(safe), run(True))
        _, (out, k5, v5, kl, vl) = lax.while_loop(lambda c: c[0], lambda c: (jnp.zeros((), jnp.bool_), run(False)), start)
        return out, k5[:, None, :], v5[:, None, :], kl[:, None, :], vl[:, None, :]

    return jax.shard_map(shard_body, mesh=mesh, in_specs=(P('cp'), P(), P(), P(), P(), P(), P(), P(), P(), P()),
                         out_specs=(P('cp'), P('cp'), P('cp'), P(), P()), check_vma=False)
```

time: 426 us -> 108 us (0.25)
  the two profiles are of different devices: /device:TPU:7 before, /device:TPU:5 now
where the time goes in v2:
time: 108 us; the launch traced here: 107 us
  Pallas kernels  94 us (87%)
  local copies, waits for them, and re-layouts  10.6 us (10%)
  between operations  1.36 us (1%)
  other arithmetic  1.3 us (1%)
    pallas_call x1, Pallas kernels, layers(): pl.pallas_call(functools.partial(layers_kernel, fast), in_specs=[pl.Block...  94 us
    unnamed x19, local copies, waits for them, and re-layouts  5.77 us
    reshape x1, local copies, waits for them, and re-layouts, shard_body(): wq = w_q.reshape(2, D, 4 * HEAD)  4.3 us

profile of v2, /device:TPU:5, one launch (start us, length us, event | category | flops | bytes accessed | tf_op | source)
XLA Modules:
  0.0 107.4 jit_solution(11017928348481745765)
XLA Ops:
  0.6 0.7 add_abs_fusion
  1.3 0.6 fusion.2
  2.6 0.5 broadcast_in_dim.15.sig_ref
  3.1 0.0 copy-start.4
  3.1 0.0 copy-start.5
  3.1 4.3 %reshape.23.wq_hbm = bf16[2,640,1024]{2,1,0:T(8,128)(2,1)S(1)} reshape(bf16[2,640,4,256]{3,2,1,0:T(4,128)(2,1)} %param.19) | data formatting | bytes 5242880 | tf_op jit(solution)/shard_map/reshape | solution.py:410
  7.4 0.0 copy-done.4
  7.4 0.0 copy-done.5
  7.4 0.0 copy-done.6
  7.5 94.0 %layers_fast.1 = (bf16[1024,640]{1,0:T(8,128)(2,1)}, bf16[1024,256]{1,0:T(8,128)(2,1)}, bf16[1024,256]{1,0:T(8,128)(2,1)}, bf16[1024,256]{1,0:T(8,128)(2,1)}, bf16[1024,256]{1,0:T(8,128)(2,1)}) custom-call(f32[2]{0:T(128)} %broadcast_in_dim.15.sig_ref, f32[2,4,640]{2,1,0:T(4,128)S(1)} %copy-done.6, f32[2,2,256]{2,1,0:T(2,128)S(1)} %copy-done.4, ...), custom_call_target="tpu_custom_call" | custom-call | flops 60000002048 | bytes 31457280 | tf_op jit(solution)/shard_map/layers_fast/pallas_call | solution.py:380
  101.4 0.2 while.19
  101.7 0.0 copy-start
  101.7 0.0 copy-start.1
  101.7 2.6 %copy.44 = bf16[1024,640]{1,0:T(8,128)(2,1)} copy(bf16[1024,640]{1,0:T(8,128)(2,1)} %get-tuple-element.331) | data formatting | bytes 2621440
  104.2 0.0 copy-done
  104.2 0.0 copy-start.2
  104.2 0.0 copy-start.3
  104.3 0.8 copy.45
  105.0 0.0 copy-done.1
  105.0 0.8 copy.46
  105.8 0.0 copy-done.2
  105.8 0.8 copy.47
  106.6 0.0 copy-done.3
  106.6 0.8 copy.48
  (2 shorter events, 0.0 us)
Async XLA Ops:
  3.1 4.3 %copy-start.4 = (f32[2,2,256]{2,1,0:T(2,128)S(1)}, f32[2,2,256]{2,1,0:T(2,128)}, u32[]{:S(2)}) copy-start(f32[2,2,256]{2,1,0:T(2,128)} %qg_ref.1) | copy-start | bytes 12292
  3.1 4.3 %copy-start.5 = (bf16[2,640,1,256]{3,1,2,0:T(8,128)(2,1)S(1)}, bf16[2,640,1,256]{3,1,2,0:T(8,128)(2,1)}, u32[]{:S(2)}) copy-start(bf16[2,640,1,256]{3,1,2,0:T(8,128)(2,1)} %param.20) | copy-start | bytes 1966084
  3.1 4.3 %copy-start.6 = (f32[2,4,640]{2,1,0:T(4,128)S(1)}, f32[2,4,640]{2,1,0:T(4,128)}, u32[]{:S(2)}) copy-start(f32[2,4,640]{2,1,0:T(4,128)} %ng_ref.1) | copy-start | bytes 61444
  101.7 2.6 %copy-start = (bf16[1024,256]{1,0:T(8,128)(2,1)S(1)}, bf16[1024,256]{1,0:T(8,128)(2,1)}, u32[]{:S(2)}) copy-start(bf16[1024,256]{1,0:T(8,128)(2,1)} %get-tuple-element.126) | copy-start | bytes 1572868
  101.7 3.4 %copy-start.1 = (bf16[1024,256]{1,0:T(8,128)(2,1)S(1)}, bf16[1024,256]{1,0:T(8,128)(2,1)}, u32[]{:S(2)}) copy-start(bf16[1024,256]{1,0:T(8,128)(2,1)} %get-tuple-element.127) | copy-start | bytes 1572868
  104.2 1.6 %copy-start.2 = (bf16[1024,256]{1,0:T(8,128)(2,1)S(1)}, bf16[1024,256]{1,0:T(8,128)(2,1)}, u32[]{:S(2)}) copy-start(bf16[1024,256]{1,0:T(8,128)(2,1)} %get-tuple-element.128) | copy-start | bytes 1572868
  104.2 2.4 %copy-start.3 = (bf16[1024,256]{1,0:T(8,128)(2,1)S(1)}, bf16[1024,256]{1,0:T(8,128)(2,1)}, u32[]{:S(2)}) copy-start(bf16[1024,256]{1,0:T(8,128)(2,1)} %get-tuple-element.129) | copy-start | bytes 1572868

commit v3 on v2

--- a/solution.py
+++ b/solution.py
@@ -75,7 +75,7 @@
 N_TILE = TOK // TILE
 QROWS = 512
 FROWS = 512
-FSTEP = 512
+FSTEP = 2048
 
 
 def finish_rows(x, attn, ng, wo, wg, wu, wd):
@@ -93,8 +93,8 @@
     return (h1.astype(F32) + rms(o2, 1.0 + ng[3:4, :])).astype(BF16)
 
 
-def layers_kernel(fast, sig_ref, ng_ref, qg_ref, hi4_ref, lo4_ref, hi5_ref, lo5_ref, x_hbm, wq_hbm, wk_hbm, wv_hbm, wo_hbm, wg_hbm, wu_hbm, wd_hbm,
-                  out_hbm, k_hbm, v_hbm, kl_hbm, vl_hbm,
+def layers_kernel(fast, ng_ref, qg_ref, hi4_ref, lo4_ref, hi5_ref, lo5_ref, x_hbm, wq_hbm, wk_hbm, wv_hbm, wo_hbm, wg_hbm, wu_hbm, wd_hbm,
+                  out_hbm, k_hbm, v_hbm, kl_hbm, vl_hbm, bound_ref,
                   x, mid, win, kv5, q, buf, acc, l, m, last, xo, wq, wk, wv, wo, wg, wu, wd,
                   load_sem, out_sem, halo_send, halo_recv, hop_send, hop_recv, pass_send, over_send, wide_recv, last_send, last_recv):
     me = lax.axis_index('cp')
@@ -144,6 +144,11 @@
     def halo_copy(t):
         return send(win.at[rows_of(t + N_TILE)], win.at[rows_of(t)], halo_send.at[t], halo_recv.at[t], (me + 1) % 8)
 
+    gains = jnp.abs(1.0 + qg_ref[...])
+    pair = jnp.maximum(gains[:, :, 0:HEAD // 2], gains[:, :, HEAD // 2:])
+    bound = 16.0 * 1.02 * jnp.max(pair[:, 0:1] * pair[:, 1:2])
+    bound_ref[0] = bound
+    sigma = jnp.maximum(bound - TOP, 0.0) * LOG2E
     g4q, g4k = 1.0 + qg_ref[0, 0:1, :], 1.0 + qg_ref[0, 1:2, :]
     g5q, g5k = 1.0 + qg_ref[1, 0:1, :], 1.0 + qg_ref[1, 1:2, :]
     for cp in early[:3]:
@@ -176,7 +181,14 @@
                 (chip == 1, hop(2, 1, 1, ynb)),
                 (chip == 2, hop(1, 3, 2, xnb))]
 
-    sig4, sig5 = sig_ref[0], sig_ref[1]
+    def early_pass(t):
+        return send(buf.at[1, rows_of(t)], buf.at[3, rows_of(t)], hop_send.at[3, t], hop_recv.at[2, t], xnb)
+
+    def first_in(t):
+        send(kv5.at[rows_of(t)], buf.at[1, rows_of(t)], hop_send.at[0, t], hop_recv.at[1, t], partner).wait_recv()
+
+    far = chip == 3
+
     n_key = WINDOW + TILE
 
     def layer_tile(it, carry):
@@ -184,7 +196,7 @@
         rows = rows_of(t)
         cos, sin = cos_sin(hi4_ref, lo4_ref, me * TOK + t * TILE, TILE)
         a = rms(x[rows, :].astype(F32), 1.0 + ng_ref[0, 0:1, :]).astype(BF16)
-        qs = [head_rope(dot(a, wq[0, :, h * HEAD:(h + 1) * HEAD]), g4q, cos, sin) for h in range(4)]
+        qs = [head_rope(dot(a, wq[0, h]), g4q, cos, sin) for h in range(4)]
 
         on(me > 0, halo_copy(t), 'wait_recv')
         start = pl.multiple_of(t * TILE, TILE)
@@ -192,7 +204,7 @@
         vs = win[pl.ds(start, n_key), HEAD:2 * HEAD]
         col = lax.broadcasted_iota(jnp.int32, (1, n_key), 1)
         hidden = jnp.logical_and(me == 0, col + start < WINDOW)
-        bias = jnp.where(hidden, NEG, -sig4 if fast else 0.0)
+        bias = jnp.where(hidden, NEG, -sigma if fast else 0.0)
         r = lax.broadcasted_iota(jnp.int32, (TILE, TILE), 0)
         c = lax.broadcasted_iota(jnp.int32, (TILE, TILE), 1)
         outs = []
@@ -211,9 +223,14 @@
         kv5[rows, 0:HEAD] = head_rope(dot(a, wk[1]), g5k, cos, sin)
         kv5[rows, HEAD:2 * HEAD] = dot(a, wv[1]).astype(BF16)
         for h in range(4):
-            q[h, rows, :] = head_rope(dot(a, wq[1, :, h * HEAD:(h + 1) * HEAD]), g5q, cos, sin)
+            q[h, rows, :] = head_rope(dot(a, wq[1, h]), g5q, cos, sin)
         for cond, cp in hops(t):
             on(cond, cp, 'start')
+
+        @pl.when(jnp.logical_and(far, it >= 1))
+        def _():
+            first_in(t + 1)
+            early_pass(t + 1).start()
         return carry
 
     lax.fori_loop(0, N_TILE, layer_tile, 0)
@@ -228,7 +245,7 @@
             vis = lax.broadcasted_iota(jnp.int32, (n, n), 1) <= r
         for h in range(4):
             s = dot_t(q[h, rows, :], ks)
-            t = s * COEF - sig5 if fast else s * COEF
+            t = s * COEF - sigma if fast else s * COEF
             if masked:
                 tail = jnp.where(vis, t[:, width - n:], NEG)
                 t = tail if width == n else jnp.concatenate([t[:, 0:width - n], tail], axis=1)
@@ -273,17 +290,16 @@
     def relay(s):
         odd = s % 2 == 1
         return [(odd, wide(s, jnp.minimum(s + 1, N_SLOT - 1), pass_send.at[s], partner)),
-                (jnp.logical_and(chip == 3, s == 1), wide(s, 3, over_send, xnb)),
                 (jnp.logical_and(jnp.logical_and(chip == 1, core == 0), s == 1), wide(s, 5, over_send, ynb)),
                 (jnp.logical_and(jnp.logical_and(chip == 2, core == 1), s == 1), wide(s, 5, over_send, xnb))]
 
-    def chunks_in(cond, slot_no, rk):
+    def chunks_in(cond, slot_no, rk, n=N_TILE):
         @pl.when(cond)
         def _():
             def one(t, carry):
                 send(kv5.at[rows_of(t)], buf.at[slot_no, rows_of(t)], hop_send.at[0, t], hop_recv.at[rk, t], partner).wait_recv()
                 return carry
-            lax.fori_loop(0, N_TILE, one, 0)
+            lax.fori_loop(0, n, one, 0)
 
     gives = jnp.logical_or(me == 3, jnp.logical_or(me == 5, me == 1))
     spread = [(gives, send(last, last, last_send.at[0], last_recv, partner)), (me == 3, send(last, last, last_send.at[1], last_recv, xnb))]
@@ -299,10 +315,15 @@
 
     def step(s, carry):
         chunks_in(jnp.logical_and(s == 0, core == 1), 0, 0)
-        chunks_in(s == 1, 1, 1)
-        chunks_in(jnp.logical_and(s == 3, chip == 3), 3, 2)
-
-        @pl.when(jnp.logical_or(jnp.logical_and(s > 0, s % 2 == 0), jnp.logical_or(s == 5, jnp.logical_and(s == 3, chip == 2))))
+        chunks_in(jnp.logical_and(s == 1, chip < 3), 1, 1)
+        chunks_in(s == 3, 3, 2)
+
+        @pl.when(jnp.logical_and(far, jnp.where(core == 1, s == 0, s == 1)))
+        def _():
+            first_in(0)
+            early_pass(0).start()
+
+        @pl.when(jnp.logical_or(jnp.logical_and(s > 0, s % 2 == 0), s == 5))
         def _():
             wide(s, s, pass_send.at[s], partner).wait_recv()
 
@@ -350,6 +371,7 @@
 
     def drain_tile(t, carry):
         on(me < top, halo_copy(t), 'wait_send')
+        on(far, early_pass(t), 'wait_send')
         for cond, cp in hops(t):
             on(cond, cp, 'wait_send')
         return carry
@@ -372,34 +394,53 @@
         out_copy(t).wait()
 
 
-def layers(fast, sig, ng, qg, rope, x, wq, wk, wv, wo, wg, wu, wd):
+def layers(fast, ng, qg, rope, x, wq, wk, wv, wo, wg, wu, wd):
     vm = pl.BlockSpec(memory_space=pltpu.VMEM)
     anyw = pl.BlockSpec(memory_space=pl.ANY)
     dma = pltpu.SemaphoreType.DMA
     kshape = jax.ShapeDtypeStruct((TOK, HEAD), BF16)
     return pl.pallas_call(
         functools.partial(layers_kernel, fast),
-        in_specs=[pl.BlockSpec(memory_space=pltpu.SMEM)] + [vm] * 6 + [anyw] * 8,
-        out_specs=[anyw] * 5,
-        out_shape=[jax.ShapeDtypeStruct((TOK, D), BF16), kshape, kshape, kshape, kshape],
+        in_specs=[vm] * 6 + [anyw] * 8,
+        out_specs=[anyw] * 5 + [pl.BlockSpec(memory_space=pltpu.SMEM)],
+        out_shape=[jax.ShapeDtypeStruct((TOK, D), BF16), kshape, kshape, kshape, kshape, jax.ShapeDtypeStruct((1,), F32)],
         scratch_shapes=[
             pltpu.VMEM((TOK, D), BF16), pltpu.VMEM((TOK, D), BF16), pltpu.VMEM((WINDOW + TOK, 2 * HEAD), BF16), pltpu.VMEM((TOK, 2 * HEAD), BF16),
             pltpu.VMEM((4, TOK, HEAD), BF16), pltpu.VMEM((N_SLOT, TOK, 2 * HEAD), BF16), pltpu.VMEM((4, TOK, HEAD), F32), pltpu.VMEM((4, TOK, 128), F32),
             pltpu.VMEM((8, 128) if fast else (4, TOK, 128), F32), pltpu.VMEM((TOK, 2 * HEAD), BF16), pltpu.VMEM((TOK, D), BF16),
-            pltpu.VMEM((2, D, 4 * HEAD), BF16), pltpu.VMEM((2, D, HEAD), BF16), pltpu.VMEM((2, D, HEAD), BF16),
+            pltpu.VMEM((2, 4, D, HEAD), BF16), pltpu.VMEM((2, D, HEAD), BF16), pltpu.VMEM((2, D, HEAD), BF16),
             pltpu.VMEM((4 * HEAD, D), BF16), pltpu.VMEM((D, FF), BF16), pltpu.VMEM((D, FF), BF16), pltpu.VMEM((FF, D), BF16),
-            dma((11,)), dma((4 + TOK // FROWS,)), dma((N_TILE,)), dma((N_TILE,)), dma((3, N_TILE)), dma((3, N_TILE)), dma((N_SLOT,)), dma, dma((N_SLOT,)),
+            dma((11,)), dma((4 + TOK // FROWS,)), dma((N_TILE,)), dma((N_TILE,)), dma((4, N_TILE)), dma((3, N_TILE)), dma((N_SLOT,)), dma, dma((N_SLOT,)),
             dma((3,)), dma],
         name="layers_fast" if fast else "layers_safe",
         compiler_params=pltpu.CompilerParams(vmem_limit_bytes=VLIM, collective_id=0 if fast else None, has_side_effects=True),
         cost_estimate=pl.CostEstimate(flops=60 * 10**9, bytes_accessed=30 << 20, transcendentals=0),
-    )(sig, ng, qg, *rope[0], *rope[1], x, wq, wk, wv, wo, wg, wu, wd)
-
-
-def score_bound(qk_gains):
-    g = jnp.abs(1.0 + qk_gains)
-    pair = jnp.maximum(g[:, :, 0:HEAD // 2], g[:, :, HEAD // 2:])
-    return 16.0 * 1.02 * jnp.max(pair[:, 0] * pair[:, 1])
+    )(ng, qg, *rope[0], *rope[1], x, wq, wk, wv, wo, wg, wu, wd)
+
+
+def emit_kernel(*refs):
+    ins, outs, mids, sem_in, sem_out = refs[0:5], refs[5:10], refs[10:15], refs[15], refs[16]
+    loads = [pltpu.make_async_copy(i, m, sem_in.at[n]) for n, (i, m) in enumerate(zip(ins, mids))]
+    stores = [pltpu.make_async_copy(m, o, sem_out.at[n]) for n, (m, o) in enumerate(zip(mids, outs))]
+    for cp in loads:
+        cp.start()
+    for ld, st in zip(loads, stores):
+        ld.wait()
+        st.start()
+    for st in stores:
+        st.wait()
+
+
+def emit(arrays):
+    anyw = pl.BlockSpec(memory_space=pl.ANY)
+    return pl.pallas_call(
+        emit_kernel,
+        in_specs=[anyw] * 5,
+        out_specs=[anyw] * 5,
+        out_shape=[jax.ShapeDtypeStruct(a.shape, a.dtype) for a in arrays],
+        scratch_shapes=[pltpu.VMEM(a.shape, a.dtype) for a in arrays] + [pltpu.SemaphoreType.DMA((5,)), pltpu.SemaphoreType.DMA((5,))],
+        name="emit",
+    )(*arrays)
 
 
 def solution(mesh):
@@ -407,19 +448,17 @@
     rope = [rope_const(layer, TOK * n_dev) for layer in range(2)]
 
     def shard_body(x, ng, qg, w_q, w_k, w_v, w_o, w_gate, w_up, w_down):
-        wq = w_q.reshape(2, D, 4 * HEAD)
+        wq = w_q.transpose(0, 2, 1, 3)
         wk = w_k.reshape(2, D, HEAD)
         wv = w_v.reshape(2, D, HEAD)
         wo = w_o.reshape(2, 4 * HEAD, D)
-        bound = score_bound(qg)
-        safe = bound <= LIMIT
-        sig = jnp.full((2,), jnp.maximum(bound - TOP, 0.0) * LOG2E)
 
         def run(fast):
-            return tuple(layers(fast, sig, ng, qg, rope, x, wq, wk, wv, wo, w_gate, w_up, w_down))
-
-        start = (jnp.logical_not(safe), run(True))
-        _, (out, k5, v5, kl, vl) = lax.while_loop(lambda c: c[0], lambda c: (jnp.zeros((), jnp.bool_), run(False)), start)
+            return tuple(layers(fast, ng, qg, rope, x, wq, wk, wv, wo, w_gate, w_up, w_down))
+
+        *first, bound = run(True)
+        _, rest = lax.while_loop(lambda c: c[0], lambda c: (jnp.zeros((), jnp.bool_), run(False)[:5]), (bound[0] > LIMIT, tuple(first)))
+        out, k5, v5, kl, vl = emit(rest)
         return out, k5[:, None, :], v5[:, None, :], kl[:, None, :], vl[:, None, :]
 
     return jax.shard_map(shard_body, mesh=mesh, in_specs=(P('cp'), P(), P(), P(), P(), P(), P(), P(), P(), P()),

time: 108 us -> 97.4 us (0.902)
  the two profiles are of different devices: /device:TPU:5 before, /device:TPU:7 now
where the time goes in v3:
time: 97.4 us; the launch traced here: 97.3 us
  Pallas kernels  93 us (95%)
  local copies, waits for them, and re-layouts  2.63 us (3%)
  between operations  1.44 us (1%)
    pallas_call x1, Pallas kernels, layers(): pl.pallas_call(functools.partial(layers_kernel, fast), in_specs=[vm] * 6...  89.9 us
    pallas_call x1, Pallas kernels, emit(): pl.pallas_call(emit_kernel, in_specs=[anyw] * 5, out_specs=[anyw] * 5, ou...  3.15 us
    unnamed x9, local copies, waits for them, and re-layouts  2.63 us

profile of v3, /device:TPU:7, one launch (start us, length us, event | category | flops | bytes accessed | tf_op | source)
XLA Modules:
  0.0 97.3 jit_solution(14200696117160560124)
XLA Ops:
  0.6 0.0 copy-start
  0.6 0.0 copy-start.2
  0.7 0.0 copy-start.3
  0.7 0.0 copy-start.4
  0.7 2.2 %copy.21 = bf16[2,640,4,256]{3,1,2,0:T(8,128)(2,1)S(1)} copy(bf16[2,640,4,256]{3,2,1,0:T(4,128)(2,1)} %param.19) | data formatting | bytes 5242880 | tf_op args[3]
  2.9 0.2 copy-done
  3.2 0.1 copy-done.2
  3.3 0.0 copy-done.3
  3.3 0.0 copy-done.4
  3.3 89.9 %layers_fast.1 = (bf16[1024,640]{1,0:T(8,128)(2,1)}, bf16[1024,256]{1,0:T(8,128)(2,1)}, bf16[1024,256]{1,0:T(8,128)(2,1)}, bf16[1024,256]{1,0:T(8,128)(2,1)}, bf16[1024,256]{1,0:T(8,128)(2,1)}, /*index=5*/f32[1]{0:T(128)}) custom-call(f32[2,4,640]{2,1,0:T(4,128)S(1)} %copy-done.3, f32[2,2,256]{2,1,0:T(2,128)S(1)} %copy-done.4, ...), custom_call_target="tpu_custom_call" | custom-call | flops 60000002048 | bytes 31457280 | tf_op jit(solution)/shard_map/layers_fast/pallas_call | solution.py:402
  93.7 0.2 while.18
  94.0 3.1 %emit.1 = (bf16[1024,640]{1,0:T(8,128)(2,1)}, bf16[1024,256]{1,0:T(8,128)(2,1)}, bf16[1024,256]{1,0:T(8,128)(2,1)}, bf16[1024,256]{1,0:T(8,128)(2,1)}, bf16[1024,256]{1,0:T(8,128)(2,1)}) custom-call(bf16[1024,640]{1,0:T(8,128)(2,1)} %get-tuple-element.289, bf16[1024,256]{1,0:T(8,128)(2,1)} %get-tuple-element.290, bf16[1024,256]{1,0:T(8,128)(2,1)} %get-tuple-element.291, ...), custom_call_target="tpu_custom_call" | custom-call | tf_op jit(solution)/shard_map/emit/pallas_call | solution.py:436
Async XLA Ops:
  0.6 2.5 %copy-start = (bf16[2,4,256,640]{3,2,1,0:T(8,128)(2,1)S(1)}, bf16[2,4,256,640]{3,2,1,0:T(8,128)(2,1)}, u32[]{:S(2)}) copy-start(bf16[2,4,256,640]{3,2,1,0:T(8,128)(2,1)} %param.22) | copy-start | bytes 7864324
  0.6 2.7 %copy-start.2 = (bf16[2,640,1,256]{3,1,2,0:T(8,128)(2,1)S(1)}, bf16[2,640,1,256]{3,1,2,0:T(8,128)(2,1)}, u32[]{:S(2)}) copy-start(bf16[2,640,1,256]{3,1,2,0:T(8,128)(2,1)} %param.20) | copy-start | bytes 1966084
  0.7 2.6 %copy-start.3 = (f32[2,4,640]{2,1,0:T(4,128)S(1)}, f32[2,4,640]{2,1,0:T(4,128)}, u32[]{:S(2)}) copy-start(f32[2,4,640]{2,1,0:T(4,128)} %ng_ref.1) | copy-start | bytes 61444
  0.7 2.6 %copy-start.4 = (f32[2,2,256]{2,1,0:T(2,128)S(1)}, f32[2,2,256]{2,1,0:T(2,128)}, u32[]{:S(2)}) copy-start(f32[2,2,256]{2,1,0:T(2,128)} %qg_ref.1) | copy-start | bytes 12292
